TPU v7x, 32 devices: a whole 2x2x4 slice. The times are simulated.
32 devices in a mesh: grp: 4 (over z), seq: 8 (over y, x, core).
Axes of the slice: x: 2, y: 2, z: 4, core: 2. Of those that a mesh axis runs over, the one named last changes fastest.
Arguments:
- hidden_in: bfloat16 [24, 4096], P(None, ('grp', 'seq')), may hold values from -6 to 6
- norm_gain: float32 [4096], replicated, may hold values from 0.5 to 1.5
- w_ssm_in: bfloat16 [4096, 8192], P(None, ('grp', 'seq')), may hold values from -0.09375 to 0.09375
- w_ssm_gate: bfloat16 [4096, 8192], P(None, ('grp', 'seq')), may hold values from -0.09375 to 0.09375
- conv_weight: float32 [4, 8192], P(None, ('grp', 'seq')), may hold values from -3 to 3
- conv_bias: float32 [8192], P(('grp', 'seq')), may hold values from -0.5 to 0.5
- conv_state: bfloat16 [24, 3, 8192], P(None, None, ('grp', 'seq')), may hold values from -6 to 6
- w_state_proj: bfloat16 [8192, 288], P(('grp', 'seq')), may hold values from -0.0625 to 0.0625
- w_step: bfloat16 [256, 8192], P(None, ('grp', 'seq')), may hold values from -0.375 to 0.375
- step_bias: float32 [8192], P(('grp', 'seq')), may hold values from -4 to -1
- log_decay: float32 [16, 8192], P(None, ('grp', 'seq')), may hold values from 0 to 2.7
- skip_gain: float32 [8192], P(('grp', 'seq')), may hold values from 0.5 to 1.5
- ssm_state: float32 [24, 16, 8192], P(None, None, ('grp', 'seq')), may hold values from -6 to 6
- w_ssm_out: bfloat16 [8192, 4096], P(('grp', 'seq')), may hold values from -0.125 to 0.125
- w_query: bfloat16 [4096, 2048], P(None, 'grp'), may hold values from -6 to 6
- key_projection: bfloat16 [4096, 1024], P(None, 'grp'), may hold values from -0.09375 to 0.09375
- value_projection: bfloat16 [4096, 1024], P(None, 'grp'), may hold values from -0.09375 to 0.09375
- w_attn_out: bfloat16 [2048, 4096], P('grp', 'seq'), may hold values from -0.125 to 0.125
- w_mlp_gate: bfloat16 [4096, 14336], P(None, ('grp', 'seq')), may hold values from -0.09375 to 0.09375
- w_mlp_up: bfloat16 [4096, 14336], P(None, ('grp', 'seq')), may hold values from -0.09375 to 0.09375
- w_mlp_down: bfloat16 [14336, 4096], P(('grp', 'seq')), may hold values from -0.09375 to 0.09375
- cached_inputs: bfloat16 [24, 512, 4096], P('seq'), may hold values from -6 to 6
- window_lengths: int32 [24], replicated, may hold values from 1 to 512, as said below
Outputs:
- hidden_out: bfloat16 [24, 4096], P(None, ('grp', 'seq'))
- state_out: float32 [24, 16, 8192], P(None, None, ('grp', 'seq'))
Inputs may be any that keep to these rules, and one draw needn't show every extreme that they name: `window_lengths`: every sequence has at least one valid cached position, and some sequence fills the whole window of 512.
All inputs are finite; a program needn't handle non-finite values.
Results may differ from a plain program's by a relative error of at most 0.012.
The roundings to bfloat16 on the way count: a program that leaves them out, or rounds other values in their place, can miss the bound.
Values may be sent and summed in bfloat16 or wider, within the bound.
A program may use at most 128 MiB of HBM per device.

v0:
```python
import functools

import jax
import jax.numpy as jnp
from jax import lax
from jax.experimental import pallas as pl
from jax.experimental.pallas import tpu as pltpu
from jax.sharding import PartitionSpec as P

HEAD_SIZE = 128
MESH = pl.DeviceIdType.MESH
VMEM_SPEC = pl.BlockSpec(memory_space=pltpu.VMEM)


epsilon = 1e-05
rope_base = 10000.0


def my_index(seq_size):
    return lax.axis_index("grp") * seq_size + lax.axis_index("seq")


def each_peer(groups, seq_size, action):
    group = lax.axis_index("grp")
    place = lax.axis_index("seq")
    group_at = [lax.rem(group + dg, groups) for dg in range(groups)]

    def step(ds, carry):
        there = lax.rem(place + ds, seq_size)
        for dg in range(groups):
            action(dg * seq_size + ds, (group_at[dg], there))
        return carry

    for dg in range(1, groups):
        action(dg * seq_size, (group_at[dg], place))
    lax.fori_loop(1, seq_size, step, 0)


def meet_all(devices, seq_size):
    barrier = pltpu.get_barrier_semaphore()
    each_peer(
        devices // seq_size,
        seq_size,
        lambda k, where: pl.semaphore_signal(
            barrier, inc=1, device_id=where, device_id_type=MESH
        ),
    )
    pl.semaphore_wait(barrier, devices - 1)


def norm_gather_kernel(devices, seq_size, x_ref, gain_ref, out_ref, buf, send_sem, recv_sem):
    me = my_index(seq_size)
    groups = devices // seq_size
    width = x_ref.shape[1]
    meet_all(devices, seq_size)

    def copy_for(k, where):
        return pltpu.make_async_remote_copy(
            src_ref=x_ref,
            dst_ref=buf.at[me],
            send_sem=send_sem.at[k],
            recv_sem=recv_sem.at[k],
            device_id=where,
            device_id_type=MESH,
        )

    each_peer(groups, seq_size, lambda k, where: copy_for(k, where).start())
    buf[me] = x_ref[...]
    each_peer(groups, seq_size, lambda k, where: copy_for(k, where).wait())
    total = jnp.zeros(x_ref.shape, jnp.float32)
    for d in range(devices):
        block = buf[d].astype(jnp.float32)
        total = total + block * block
    scale = lax.rsqrt(
        jnp.sum(total, axis=1, keepdims=True) * (1.0 / (devices * width)) + epsilon
    )
    for d in range(devices):
        cols = slice(d * width, (d + 1) * width)
        out_ref[:, cols] = (buf[d].astype(jnp.float32) * scale * gain_ref[:, cols]).astype(
            jnp.bfloat16
        )


def norm_gather(devices, seq_size, hidden_in, norm_gain):
    rows, width = hidden_in.shape
    return pl.pallas_call(
        functools.partial(norm_gather_kernel, devices, seq_size),
        out_shape=jax.ShapeDtypeStruct((rows, devices * width), jnp.bfloat16),
        in_specs=[VMEM_SPEC] * 2,
        out_specs=VMEM_SPEC,
        scratch_shapes=[
            pltpu.VMEM((devices, rows, width), jnp.bfloat16),
            pltpu.SemaphoreType.DMA((devices,)),
            pltpu.SemaphoreType.DMA((devices,)),
        ],
        compiler_params=pltpu.CompilerParams(
            collective_id=0, has_side_effects=True, vmem_limit_bytes=8 * 1024 * 1024
        ),
        cost_estimate=pl.CostEstimate(
            flops=2_000_000_000, bytes_accessed=30_000_000, transcendentals=0
        ),
    )(hidden_in, norm_gain.reshape(1, -1))


def sum_gather_kernel(
    devices,
    seq_size,
    part_ref,
    att_ref,
    out_ref,
    att_out_ref,
    split,
    landed,
    reduced,
    full,
    att_buf,
    send_sem,
    recv_sem,
    send_all_sem,
    recv_all_sem,
    att_send_sem,
    att_recv_sem,
):
    me = my_index(seq_size)
    groups = devices // seq_size
    group = lax.axis_index("grp")
    place = lax.axis_index("seq")
    owners, each = split.shape[0], split.shape[1]
    own_rows = att_ref.shape[0]
    for r in range(owners):
        split[r] = part_ref[r * each : (r + 1) * each, :]
    meet_all(devices, seq_size)

    def index_of(where):
        return where[0] * seq_size + where[1]

    def part_copy(k, where):
        return pltpu.make_async_remote_copy(
            src_ref=split.at[index_of(where)],
            dst_ref=landed.at[me],
            send_sem=send_sem.at[k],
            recv_sem=recv_sem.at[k],
            device_id=where,
            device_id_type=MESH,
        )

    def land_copy(k, where):
        return pltpu.make_async_remote_copy(
            src_ref=reduced,
            dst_ref=landed.at[me],
            send_sem=send_sem.at[k],
            recv_sem=recv_sem.at[k],
            device_id=where,
            device_id_type=MESH,
        )

    def full_copy(k, where):
        return pltpu.make_async_remote_copy(
            src_ref=reduced,
            dst_ref=full.at[me],
            send_sem=send_all_sem.at[k],
            recv_sem=recv_all_sem.at[k],
            device_id=where,
            device_id_type=MESH,
        )

    def att_copy(k):
        return pltpu.make_async_remote_copy(
            src_ref=att_ref,
            dst_ref=att_buf.at[place],
            send_sem=att_send_sem.at[k],
            recv_sem=att_recv_sem.at[k],
            device_id=(group, lax.rem(place + k, seq_size)),
            device_id_type=MESH,
        )

    def each_place(action):
        def step(k, carry):
            action(k)
            return carry

        lax.fori_loop(1, seq_size, step, 0)

    def start_part(k, where):
        @pl.when(index_of(where) < owners)
        def _():
            part_copy(k, where).start()

    each_peer(groups, seq_size, start_part)
    each_place(lambda k: att_copy(k).start())
    att_buf[place] = att_ref[...]

    @pl.when(me < owners)
    def _():
        landed[me] = split[me]
        each_peer(groups, seq_size, lambda k, where: land_copy(k, where).wait_recv())
        total = landed[0]
        for d in range(1, devices):
            total = total + landed[d]
        reduced[...] = total
        full[me] = total
        each_peer(groups, seq_size, lambda k, where: full_copy(k, where).start())

    def end_part(k, where):
        @pl.when(index_of(where) < owners)
        def _():
            part_copy(k, where).wait_send()

    each_peer(groups, seq_size, end_part)
    each_place(lambda k: att_copy(k).wait())
    for s in range(seq_size):
        att_out_ref[s * own_rows : (s + 1) * own_rows, :] = att_buf[s]

    def end_full(ds, carry):
        there = lax.rem(place + seq_size - ds, seq_size)
        for dg in range(groups):
            source = lax.rem(group + groups - dg, groups) * seq_size + there
            k = dg * seq_size + ds

            @pl.when(jnp.logical_and(source < owners, k > 0))
            def _():
                pltpu.make_async_remote_copy(
                    src_ref=reduced,
                    dst_ref=full.at[source],
                    send_sem=send_all_sem.at[k],
                    recv_sem=recv_all_sem.at[k],
                    device_id=(group, lax.rem(place + 1, seq_size)),
                    device_id_type=MESH,
                ).wait_recv()

        return carry

    lax.fori_loop(0, seq_size, end_full, 0)

    @pl.when(me < owners)
    def _():
        each_peer(groups, seq_size, lambda k, where: full_copy(k, where).wait_send())

    for r in range(owners):
        out_ref[r * each : (r + 1) * each, :] = full[r]


def sum_gather(devices, seq_size, part, att):
    rows, width = part.shape
    each = -(-rows // devices)
    while rows % each:
        each += 1
    owners = rows // each
    dma = pltpu.SemaphoreType.DMA
    return pl.pallas_call(
        functools.partial(sum_gather_kernel, devices, seq_size),
        out_shape=(
            jax.ShapeDtypeStruct((rows, width), jnp.float32),
            jax.ShapeDtypeStruct((seq_size * att.shape[0], att.shape[1]), jnp.float32),
        ),
        in_specs=[VMEM_SPEC] * 2,
        out_specs=(VMEM_SPEC, VMEM_SPEC),
        scratch_shapes=[
            pltpu.VMEM((owners, each, width), jnp.float32),
            pltpu.VMEM((devices, each, width), jnp.float32),
            pltpu.VMEM((each, width), jnp.float32),
            pltpu.VMEM((owners, each, width), jnp.float32),
            pltpu.VMEM((seq_size,) + att.shape, jnp.float32),
            dma((devices,)),
            dma((devices,)),
            dma((devices,)),
            dma((devices,)),
            dma((seq_size,)),
            dma((seq_size,)),
        ],
        compiler_params=pltpu.CompilerParams(
            collective_id=1, has_side_effects=True, vmem_limit_bytes=8 * 1024 * 1024
        ),
        cost_estimate=pl.CostEstimate(
            flops=2_000_000_000, bytes_accessed=30_000_000, transcendentals=0
        ),
    )(part, att)


def scatter_sum_kernel(
    devices, seq_size, term_ref, hidden_ref, out_ref, outgoing, landed, send_sem, recv_sem
):
    me = my_index(seq_size)
    groups = devices // seq_size
    width = hidden_ref.shape[1]
    for d in range(devices):
        outgoing[d] = term_ref[:, d * width : (d + 1) * width].astype(jnp.bfloat16)
    meet_all(devices, seq_size)

    def copy_for(k, where):
        return pltpu.make_async_remote_copy(
            src_ref=outgoing.at[where[0] * seq_size + where[1]],
            dst_ref=landed.at[me],
            send_sem=send_sem.at[k],
            recv_sem=recv_sem.at[k],
            device_id=where,
            device_id_type=MESH,
        )

    each_peer(groups, seq_size, lambda k, where: copy_for(k, where).start())
    landed[me] = outgoing[me]
    each_peer(groups, seq_size, lambda k, where: copy_for(k, where).wait())
    total = landed[0].astype(jnp.float32)
    for d in range(1, devices):
        total = total + landed[d].astype(jnp.float32)
    out_ref[...] = (hidden_ref[...].astype(jnp.float32) + total).astype(jnp.bfloat16)


def scatter_sum(devices, seq_size, term, hidden_in):
    rows, width = hidden_in.shape
    return pl.pallas_call(
        functools.partial(scatter_sum_kernel, devices, seq_size),
        out_shape=jax.ShapeDtypeStruct((rows, width), jnp.bfloat16),
        in_specs=[VMEM_SPEC] * 2,
        out_specs=VMEM_SPEC,
        scratch_shapes=[
            pltpu.VMEM((devices, rows, width), jnp.bfloat16),
            pltpu.VMEM((devices, rows, width), jnp.bfloat16),
            pltpu.SemaphoreType.DMA((devices,)),
            pltpu.SemaphoreType.DMA((devices,)),
        ],
        compiler_params=pltpu.CompilerParams(
            collective_id=2, has_side_effects=True, vmem_limit_bytes=8 * 1024 * 1024
        ),
        cost_estimate=pl.CostEstimate(
            flops=2_000_000_000, bytes_accessed=30_000_000, transcendentals=0
        ),
    )(term, hidden_in)


def window_kernel(
    own,
    kv_here,
    heads_per_group,
    normed_ref,
    cos_ref,
    sin_ref,
    cos_new_ref,
    sin_new_ref,
    bias_ref,
    cached_ref,
    wk_ref,
    wv_ref,
    wq_ref,
    out_ref,
    x_buf,
    wkv,
    wq,
    k_buf,
    v_buf,
    new_rows,
    x_sem,
    w_sem,
):
    tiles, tile = x_buf.shape[0], x_buf.shape[1]
    per_seq = tiles // own
    window = per_seq * tile
    kv_width = kv_here * HEAD_SIZE
    q_width = wq.shape[1]
    copy_k = pltpu.make_async_copy(wk_ref, wkv.at[:, pl.ds(0, kv_width)], w_sem.at[0])
    copy_v = pltpu.make_async_copy(wv_ref, wkv.at[:, pl.ds(kv_width, kv_width)], w_sem.at[1])
    copy_q = pltpu.make_async_copy(wq_ref, wq, w_sem.at[2])
    copy_k.start()
    copy_v.start()
    for t in range(tiles):
        pltpu.make_async_copy(cached_ref.at[t], x_buf.at[t], x_sem.at[t]).start()
    copy_q.start()
    copy_k.wait()
    copy_v.wait()

    def turned(values, cosine, sine):
        return (values * cosine + pltpu.roll(values, HEAD_SIZE // 2, 1) * sine).astype(
            jnp.bfloat16
        )

    def project(t, carry):
        pltpu.make_async_copy(cached_ref.at[t], x_buf.at[t], x_sem.at[t]).wait()
        rows = jnp.dot(x_buf[t], wkv[...], preferred_element_type=jnp.float32)
        slots = pl.ds(pl.multiple_of(lax.rem(t, per_seq) * tile, tile), tile)
        cosine, sine = cos_ref[slots, :], sin_ref[slots, :]
        here = pl.ds(pl.multiple_of(t * tile, tile), tile)
        for h in range(kv_here):
            cols = slice(h * HEAD_SIZE, (h + 1) * HEAD_SIZE)
            k_buf[here, cols] = turned(rows[:, cols], cosine, sine)
        v_buf[here, :] = rows[:, kv_width:].astype(jnp.bfloat16)
        return carry

    lax.fori_loop(0, tiles, project, 0)
    copy_q.wait()
    normed = normed_ref[...]
    new_rows[:, :q_width] = jnp.dot(normed, wq[...], preferred_element_type=jnp.float32)
    new_rows[:, q_width:] = jnp.dot(normed, wkv[...], preferred_element_type=jnp.float32)
    first = lax.axis_index("seq") * own
    scale = HEAD_SIZE ** (-0.5)
    for b in range(own):
        row = new_rows[pl.ds(first + b, 1), :]
        cosine, sine = cos_new_ref[b : b + 1, :], sin_new_ref[b : b + 1, :]
        here = slice(b * window, (b + 1) * window)
        for h in range(kv_here):
            cols = slice(h * HEAD_SIZE, (h + 1) * HEAD_SIZE)
            heads = range(h * heads_per_group, (h + 1) * heads_per_group)
            query = turned(
                jnp.concatenate(
                    [row[:, q * HEAD_SIZE : (q + 1) * HEAD_SIZE] for q in heads], axis=0
                ),
                cosine,
                sine,
            )
            at = q_width + h * HEAD_SIZE
            fresh_key = turned(row[:, at : at + HEAD_SIZE], cosine, sine)
            at += kv_width
            fresh_value = row[:, at : at + HEAD_SIZE].astype(jnp.bfloat16).astype(jnp.float32)
            scores = lax.dot_general(
                query,
                k_buf[here, cols],
                (((1,), (1,)), ((), ())),
                preferred_element_type=jnp.float32,
            )
            scores = scores * scale + bias_ref[b : b + 1, :]
            fresh = (
                jnp.sum(
                    query.astype(jnp.float32) * fresh_key.astype(jnp.float32),
                    axis=1,
                    keepdims=True,
                )
                * scale
            )
            top = jnp.maximum(jnp.max(scores, axis=1, keepdims=True), fresh)
            weights = jnp.exp(scores - top)
            weight_new = jnp.exp(fresh - top)
            total = jnp.sum(weights, axis=1, keepdims=True) + weight_new
            mixed = jnp.dot(
                weights.astype(jnp.bfloat16), v_buf[here, cols], preferred_element_type=jnp.float32
            )
            mixed = (mixed + weight_new * fresh_value) / total
            mixed = mixed.astype(jnp.bfloat16).astype(jnp.float32)
            for i, q in enumerate(heads):
                out_ref[b : b + 1, q * HEAD_SIZE : (q + 1) * HEAD_SIZE] = mixed[i : i + 1, :]


def rotary_tables(positions):
    half_dim = HEAD_SIZE // 2
    frequency = rope_base ** (-(jnp.arange(half_dim, dtype=jnp.float32) * 2.0) / HEAD_SIZE)
    angles = positions[:, None] * frequency
    cosine, sine = jnp.cos(angles), jnp.sin(angles)
    return (
        jnp.concatenate([cosine, cosine], axis=1),
        jnp.concatenate([-sine, sine], axis=1),
    )


def window_attention(normed, cached, wk, wv, wq, lengths):
    own, window, width = cached.shape
    tile = 256 if window % 256 == 0 else window
    tiles = own * window // tile
    kv_width, q_width = wk.shape[1], wq.shape[1]
    slots = jnp.arange(window, dtype=jnp.int32)
    cosine, sine = rotary_tables(slots.astype(jnp.float32))
    cos_new, sin_new = rotary_tables(lengths.astype(jnp.float32))
    bias = jnp.where(slots[None, :] < lengths[:, None], 0.0, -1e30).astype(jnp.float32)
    any_spec = pl.BlockSpec(memory_space=pl.ANY)
    return pl.pallas_call(
        functools.partial(
            window_kernel, own, kv_width // HEAD_SIZE, q_width // kv_width
        ),
        out_shape=jax.ShapeDtypeStruct((own, q_width), jnp.float32),
        in_specs=[VMEM_SPEC] * 6 + [any_spec] * 4,
        out_specs=VMEM_SPEC,
        scratch_shapes=[
            pltpu.VMEM((tiles, tile, width), jnp.bfloat16),
            pltpu.VMEM((width, 2 * kv_width), jnp.bfloat16),
            pltpu.VMEM((width, q_width), jnp.bfloat16),
            pltpu.VMEM((own * window, kv_width), jnp.bfloat16),
            pltpu.VMEM((own * window, kv_width), jnp.bfloat16),
            pltpu.VMEM((normed.shape[0], q_width + 2 * kv_width), jnp.float32),
            pltpu.SemaphoreType.DMA((tiles,)),
            pltpu.SemaphoreType.DMA((3,)),
        ],
        compiler_params=pltpu.CompilerParams(vmem_limit_bytes=48 * 1024 * 1024),
    )(normed, cosine, sine, cos_new, sin_new, bias, cached.reshape(tiles, tile, width), wk, wv, wq)


def per_device(
    devices,
    seq_size,
    hidden_in,
    norm_gain,
    w_ssm_in,
    w_ssm_gate,
    conv_weight,
    conv_bias,
    conv_state,
    w_state_proj,
    w_step,
    step_bias,
    log_decay,
    skip_gain,
    ssm_state,
    w_ssm_out,
    w_query,
    key_projection,
    value_projection,
    w_attn_out,
    w_mlp_gate,
    w_mlp_up,
    w_mlp_down,
    cached_inputs,
    window_lengths,
):
    batch_rows = hidden_in.shape[0]
    model_width = norm_gain.shape[0]
    normed_input = norm_gather(devices, seq_size, hidden_in, norm_gain)
    ssm_input = jnp.dot(normed_input, w_ssm_in, preferred_element_type=jnp.float32).astype(
        jnp.bfloat16
    )
    gate_input = jnp.dot(normed_input, w_ssm_gate, preferred_element_type=jnp.float32)
    past_inputs = conv_state.astype(jnp.float32)
    conv_sum = (
        conv_bias
        + jnp.sum(past_inputs * conv_weight[:-1][None], axis=1)
        + conv_weight[-1] * lax.optimization_barrier(ssm_input).astype(jnp.float32)
    )
    conv_out = jax.nn.silu(conv_sum)
    rank_size = w_step.shape[0]
    state_size = log_decay.shape[0]
    low_rank_part = jnp.dot(
        conv_out.astype(jnp.bfloat16), w_state_proj, preferred_element_type=jnp.float32
    )
    own_seqs = cached_inputs.shape[0]
    seq_start = lax.axis_index("seq") * own_seqs
    lengths_own = lax.dynamic_slice_in_dim(window_lengths, seq_start, own_seqs, 0)
    attended_own = window_attention(
        normed_input, cached_inputs, key_projection, value_projection, w_query, lengths_own
    )
    low_rank, attended = sum_gather(devices, seq_size, low_rank_part, attended_own)
    step_low = low_rank[:, :rank_size].astype(jnp.bfloat16)
    input_map = low_rank[:, rank_size : rank_size + state_size]
    output_map = low_rank[:, rank_size + state_size :]
    step_size = jax.nn.softplus(
        jnp.dot(step_low, w_step, preferred_element_type=jnp.float32) + step_bias
    )
    decay_rate = jnp.exp(log_decay)
    state_out = (
        jnp.exp(-step_size[:, None, :] * decay_rate[None]) * ssm_state
        + step_size[:, None, :] * input_map[:, :, None] * conv_out[:, None, :]
    )
    ssm_mixed = jnp.sum(state_out * output_map[:, :, None], axis=1) + skip_gain * conv_out
    ssm_gated = (ssm_mixed * jax.nn.silu(gate_input)).astype(jnp.bfloat16)
    ssm_term = jnp.dot(ssm_gated, w_ssm_out, preferred_element_type=jnp.float32)
    gate_act = jnp.dot(normed_input, w_mlp_gate, preferred_element_type=jnp.float32)
    up_act = jnp.dot(normed_input, w_mlp_up, preferred_element_type=jnp.float32)
    mlp_hidden = (jax.nn.silu(gate_act) * up_act).astype(jnp.bfloat16)
    mlp_term = jnp.dot(mlp_hidden, w_mlp_down, preferred_element_type=jnp.float32)
    attn_cols = jnp.dot(attended.astype(jnp.bfloat16), w_attn_out, preferred_element_type=jnp.float32)
    col_start = lax.axis_index("seq") * w_attn_out.shape[1]
    attn_term = lax.dynamic_update_slice(
        jnp.zeros((batch_rows, model_width), jnp.float32), attn_cols, (jnp.int32(0), col_start)
    )
    hidden_out = scatter_sum(devices, seq_size, ssm_term + mlp_term + attn_term, hidden_in)
    return (hidden_out, state_out)


def solution(mesh):
    placed = (
        P(None, ("grp", "seq")),
        P(),
        P(None, ("grp", "seq")),
        P(None, ("grp", "seq")),
        P(None, ("grp", "seq")),
        P(("grp", "seq")),
        P(None, None, ("grp", "seq")),
        P(("grp", "seq"), None),
        P(None, ("grp", "seq")),
        P(("grp", "seq")),
        P(None, ("grp", "seq")),
        P(("grp", "seq")),
        P(None, None, ("grp", "seq")),
        P(("grp", "seq"), None),
        P(None, "grp"),
        P(None, "grp"),
        P(None, "grp"),
        P("grp", "seq"),
        P(None, ("grp", "seq")),
        P(None, ("grp", "seq")),
        P(("grp", "seq"), None),
        P("seq", None, None),
        P(),
    )
    return jax.shard_map(
        functools.partial(per_device, mesh.size, mesh.shape["seq"]),
        mesh=mesh,
        in_specs=placed,
        out_specs=(P(None, ("grp", "seq")), P(None, None, ("grp", "seq"))),
        check_vma=False,
    )
```

profile of v0, /device:TPU:0, one launch (start us, length us, event | category | flops | bytes accessed | tf_op | source)
XLA Modules:
  0.0 69.6 jit_solution(17544884470797511578)
XLA Ops:
  0.6 0.0 copy-start
  0.6 0.9 %fusion.19 = (f32[3]{0:T(128)S(1)}, s32[3]{0:T(128)S(1)}) fusion(s32[24]{0:T(128)} %param.45, s32[]{:T(128)S(6)} %select_n.14), kind=kLoop, calls=%fused_computation.42 | loop fusion | flops 3 | bytes 40 | tf_op jit(solution)/shard_map/convert_element_type | solution.py:459
  1.5 0.1 fusion.18
  1.7 0.1 pad_maximum_fusion.2
  1.7 1.0 %fusion.2 = (f32[512,64]{1,0:T(8,128)S(1)}, f32[512,64]{1,0:T(8,128)S(1)}, f32[512,64]{1,0:T(8,128)S(1)}) fusion(f32[64]{0:T(128)S(1)} %multiply_power_fusion, f32[512]{0:T(512)S(1)} %iota_convert_fusion), kind=kLoop, calls=%fused_computation.13 | loop fusion | flops 65536 | bytes 395520 | tf_op jit(solution)/shard_map/neg | solution.py:448
  2.7 0.2 pad_maximum_fusion
  3.0 0.1 fusion.15.bias_ref
  3.0 0.0 copy-start.3
  3.0 0.7 %copy-done.3 = f32[4096]{0:T(1024)S(1)} copy-done((f32[4096]{0:T(1024)S(1)}, f32[4096]{0:T(1024)}, u32[]{:S(2)}) %copy-start.3) | copy-done | bytes 16408
  3.7 0.0 copy-start.4
  3.7 0.7 copy-done.4
  4.4 13.3 %shard_map.230.normed_ref = bf16[24,4096]{1,0:T(8,128)(2,1)S(1)} custom-call(bf16[24,128]{1,0:T(8,128)(2,1)S(1)} %copy-done.4, f32[1,4096]{1,0:T(1,128)S(1)} %bitcast.17), custom_call_target="tpu_custom_call" | custom-call | flops 2000000000 | bytes 30000000 | tf_op jit(solution)/shard_map/pallas_call | solution.py:86
  17.8 0.0 copy-done.1
  17.8 0.0 copy-done.2
  17.8 0.0 copy-start.6
  17.8 0.0 copy-start.10
  17.8 0.0 copy-start.12
  17.8 0.0 copy-start.13
  17.8 0.0 copy-start.8
  17.9 13.3 %shard_map.231.att_ref = f32[3,512]{1,0:T(4,128)S(1)} custom-call(bf16[24,4096]{1,0:T(8,128)(2,1)S(1)} %shard_map.230.normed_ref, f32[512,128]{1,0:T(8,128)S(1)} %get-tuple-element.20.cos_ref, f32[512,128]{1,0:T(8,128)S(1)} %get-tuple-element.21.sin_ref, f32[3,128]{1,0:T(4,128)S(1)} %get-tuple-element.22.cos_new_ref, ...), custom_call_target="tpu_custom_call" | custom-call | tf_op jit(solution)/shard_map/pallas_call | solution.py:462
  31.1 0.0 copy-done.6
  31.1 0.4 convolution_convert_fusion
  31.5 0.0 copy-done.10
  31.5 0.0 copy-done.12
  31.6 0.0 copy-done.13
  31.6 0.0 copy-done.8
  31.6 0.2 fusion.12.part_ref
  31.8 0.0 copy-start.11
  31.8 0.0 copy-start.7
  31.8 0.0 copy-start.15
  31.8 13.9 %shard_map.232 = (f32[24,288]{1,0:T(8,128)S(1)}, f32[24,512]{1,0:T(8,128)S(1)}) custom-call(f32[24,288]{1,0:T(8,128)S(1)} %fusion.12.part_ref, f32[3,512]{1,0:T(4,128)S(1)} %shard_map.231.att_ref), custom_call_target="tpu_custom_call" | custom-call | flops 2000000000 | bytes 30000000 | tf_op jit(solution)/shard_map/pallas_call | solution.py:250
  45.7 0.0 copy-done.9
  45.7 0.0 copy-done.14
  45.7 0.2 fusion.21
  45.9 0.1 fusion.20
  46.0 0.0 copy-done.11
  46.0 0.0 copy-done.7
  46.0 0.9 %multiply_reduce_fusion = (f32[24,256]{1,0:T(8,128)S(1)}, f32[24,16,256]{2,1,0:T(8,128)}) fusion(f32[24,16]{1,0:T(8,128)S(1)} %get-tuple-element.11, f32[24,256]{1,0:T(8,128)S(1)} %divide_multiply_fusion, f32[24,16]{1,0:T(8,128)S(1)} %get-tuple-element.10, f32[24,256]{1,0:T(8,128)S(1)} %get-tuple-element.19, f32[24,16,256]{2,1,0:T(8,128)S(1)} %copy-done.7, ...), kind=kLoop, calls=%fused_computation.7 | loop fusion | flops 681984 | bytes 904192 | tf_op jit(solution)/shard_map/reduce_sum | solution.py:547
  46.9 0.0 copy-done
  46.9 0.0 copy-done.15
  46.9 2.9 %fusion.10 = f32[24,4096]{1,0:T(8,128)S(1)} fusion(bf16[256,4096]{1,0:T(8,128)(2,1)S(1)} %copy-done, f32[24,256]{1,0:T(8,128)S(1)} %get-tuple-element.6, f32[24,256]{1,0:T(8,128)S(1)} %divide_multiply_fusion, f32[256]{0:T(256)S(1)} %copy-done.15, bf16[24,4096]{1,0:T(8,128)(2,1)S(1)} %shard_map.230.normed_ref, bf16[4096,256]{1,0:T(8,128)(2,1)} %param.26), kind=kOutput, calls=%fused_computation.26 | convolution fusion | flops 100712448 | bytes 4834304 | tf_op jit(solution)/shard_map/dot_general | solution.py:549
  49.8 3.1 %fusion.24 = f32[24,448]{1,0:T(8,128)S(1)} fusion(bf16[24,4096]{1,0:T(8,128)(2,1)S(1)} %shard_map.230.normed_ref, bf16[4096,448]{0,1:T(8,128)(2,1)} %param.41), kind=kOutput, calls=%fused_computation.46 | convolution fusion | flops 88080384 | bytes 3909632 | tf_op jit(solution)/shard_map/dot_general | solution.py:550
  52.9 0.0 copy-start.5
  53.0 5.1 %convolution_add_fusion = f32[24,4096]{1,0:T(8,128)S(1)} fusion(f32[24,4096]{1,0:T(8,128)S(1)} %fusion.10, bf16[448,4096]{1,0:T(8,128)(2,1)} %param.43, bf16[24,4096]{1,0:T(8,128)(2,1)S(1)} %shard_map.230.normed_ref, bf16[4096,448]{0,1:T(8,128)(2,1)} %param.42, f32[24,448]{1,0:T(8,128)S(1)} %fusion.24), kind=kOutput, calls=%fused_computation | convolution fusion | flops 176323584 | bytes 8366080 | tf_op jit(solution)/shard_map/dot_general | solution.py:553
  58.0 1.2 %fusion.term_ref = f32[24,4096]{1,0:T(8,128)S(1)} fusion(f32[24,4096]{1,0:T(8,128)S(1)} %convolution_add_fusion, s32[]{:T(128)S(6)} %select_n.17, bf16[512,512]{1,0:T(8,128)(2,1)} %param.40, f32[24,512]{1,0:T(8,128)S(1)} %get-tuple-element.5), kind=kOutput, calls=%fused_computation.3 | convolution fusion | flops 12607488 | bytes 671748 | tf_op jit(solution)/shard_map/dot_general | solution.py:554
  59.3 0.0 copy-done.5
  59.3 9.8 %shard_map.233 = bf16[24,128]{1,0:T(8,128)(2,1)S(1)} custom-call(f32[24,4096]{1,0:T(8,128)S(1)} %fusion.term_ref, bf16[24,128]{1,0:T(8,128)(2,1)S(1)} %copy-done.5), custom_call_target="tpu_custom_call" | custom-call | flops 2000000000 | bytes 30000000 | tf_op jit(solution)/shard_map/pallas_call | solution.py:311
  69.0 0.6 copy.27
  (10 shorter events, 0.1 us)
Async XLA Ops:
  0.6 46.3 %copy-start = (bf16[256,4096]{1,0:T(8,128)(2,1)S(1)}, bf16[256,4096]{1,0:T(8,128)(2,1)}, u32[]{:S(2)}) copy-start(bf16[256,4096]{1,0:T(8,128)(2,1)} %param.36) | copy-start | bytes 6291460
  3.0 0.7 %copy-start.3 = (f32[4096]{0:T(1024)S(1)}, f32[4096]{0:T(1024)}, u32[]{:S(2)}) copy-start(f32[4096]{0:T(1024)} %param.24) | copy-start | bytes 49156
  3.7 0.7 copy-start.4
  4.4 13.3 %copy-start.1 = (bf16[4096,256]{1,0:T(8,128)(2,1)S(1)}, bf16[4096,256]{1,0:T(8,128)(2,1)}, u32[]{:S(2)}) copy-start(bf16[4096,256]{1,0:T(8,128)(2,1)} %wk_ref.1) | copy-start | bytes 6291460
  4.4 13.3 %copy-start.2 = (bf16[4096,256]{1,0:T(8,128)(2,1)S(1)}, bf16[4096,256]{1,0:T(8,128)(2,1)}, u32[]{:S(2)}) copy-start(bf16[4096,256]{1,0:T(8,128)(2,1)} %wv_ref.1) | copy-start | bytes 6291460
  17.8 13.3 %copy-start.6 = (bf16[4096,256]{1,0:T(8,128)(2,1)S(1)}, bf16[4096,256]{1,0:T(8,128)(2,1)}, u32[]{:S(2)}) copy-start(bf16[4096,256]{1,0:T(8,128)(2,1)} %param.25) | copy-start | bytes 6291460
  17.8 13.7 %copy-start.10 = (bf16[24,3,256]{2,0,1:T(8,128)(2,1)S(1)}, bf16[24,3,256]{2,0,1:T(8,128)(2,1)}, u32[]{:S(2)}) copy-start(bf16[24,3,256]{2,0,1:T(8,128)(2,1)} %param.29) | copy-start | bytes 110596
  17.8 13.7 %copy-start.12 = (f32[4,256]{1,0:T(4,128)S(1)}, f32[4,256]{1,0:T(4,128)}, u32[]{:S(2)}) copy-start(f32[4,256]{1,0:T(4,128)} %param.27) | copy-start | bytes 12292
  17.8 13.7 %copy-start.13 = (f32[256]{0:T(256)S(1)}, f32[256]{0:T(256)}, u32[]{:S(2)}) copy-start(f32[256]{0:T(256)} %param.28) | copy-start | bytes 3076
  17.8 13.8 %copy-start.8 = (bf16[256,288]{0,1:T(8,128)(2,1)S(1)}, bf16[256,288]{0,1:T(8,128)(2,1)}, u32[]{:S(2)}) copy-start(bf16[256,288]{0,1:T(8,128)(2,1)} %param.30) | copy-start | bytes 442372
  31.8 13.9 %copy-start.9 = (bf16[256,256]{1,0:T(8,128)(2,1)S(1)}, bf16[256,256]{1,0:T(8,128)(2,1)}, u32[]{:S(2)}) copy-start(bf16[256,256]{1,0:T(8,128)(2,1)} %param.31) | copy-start | bytes 393220
  31.8 13.9 %copy-start.14 = (f32[256]{0:T(256)S(1)}, f32[256]{0:T(256)}, u32[]{:S(2)}) copy-start(f32[256]{0:T(256)} %param.32) | copy-start | bytes 3076
  31.8 14.2 %copy-start.11 = (f32[16,256]{1,0:T(8,128)S(1)}, f32[16,256]{1,0:T(8,128)}, u32[]{:S(2)}) copy-start(f32[16,256]{1,0:T(8,128)} %param.33) | copy-start | bytes 49156
  31.8 14.2 %copy-start.7 = (f32[24,16,256]{2,1,0:T(8,128)S(1)}, f32[24,16,256]{2,1,0:T(8,128)}, u32[]{:S(2)}) copy-start(f32[24,16,256]{2,1,0:T(8,128)} %param.35) | copy-start | bytes 1179652
  31.8 15.1 %copy-start.15 = (f32[256]{0:T(256)S(1)}, f32[256]{0:T(256)}, u32[]{:S(2)}) copy-start(f32[256]{0:T(256)} %param.34) | copy-start | bytes 3076
  52.9 6.3 %copy-start.5 = (bf16[24,128]{1,0:T(8,128)(2,1)S(1)}, bf16[24,128]{1,0:T(8,128)(2,1)}, u32[]{:S(2)}) copy-start(bf16[24,128]{1,0:T(8,128)(2,1)} %hidden_ref.1) | copy-start | bytes 18436
where the time goes:
time: 70 us; the launch traced here: 69.6 us
  Pallas kernels  50.2 us (72%)
  matrix products  13 us (19%)
  other arithmetic  3.32 us (5%)
  local copies, waits for them, and re-layouts  2.21 us (3%)
  between operations  0.89 us (1%)
    pallas_call x1, Pallas kernels, sum_gather(): pl.pallas_call(functools.partial(sum_gather_kernel, devices, seq_size), o...  13.9 us
    pallas_call x1, Pallas kernels, norm_gather(): pl.pallas_call(functools.partial(norm_gather_kernel, devices, seq_size),...  13.3 us
    pallas_call x1, Pallas kernels, window_attention(): pl.pallas_call(functools.partial(window_kernel, own, kv_width // HEAD_SIZ...  13.3 us
    pallas_call x1, Pallas kernels, scatter_sum(): pl.pallas_call(functools.partial(scatter_sum_kernel, devices, seq_size),...  9.75 us
    dot_general x1, matrix products, per_device(): jnp.dot(mlp_hidden, w_mlp_down, preferred_element_type=jnp.float32)  5.08 us
    dot_general x1, matrix products, per_device(): jnp.dot(normed_input, w_mlp_gate, preferred_element_type=jnp.float32)  3.12 us
    dot_general x1, matrix products, per_device(): ssm_term = jnp.dot(ssm_gated, w_ssm_out, preferred_element_type=jnp.float32)  2.88 us
    unnamed x33, local copies, waits for them, and re-layouts  2.13 us

commit v1 on v0

v1 whole, which is shorter than its diff:
```python
import functools

import jax
import jax.numpy as jnp
import numpy as np
from jax import lax
from jax.experimental import pallas as pl
from jax.experimental.pallas import tpu as pltpu
from jax.sharding import PartitionSpec as P

HEAD_SIZE = 128
MESH = pl.DeviceIdType.MESH
VMEM_LIMIT = 66_000_000

epsilon = 1e-05
rope_base = 10000.0

bf16 = jnp.bfloat16
f32 = jnp.float32


def dot_nn(a, b):
    return jnp.dot(a, b, preferred_element_type=f32)


def dot_nt(a, b):
    return lax.dot_general(a, b, (((1,), (1,)), ((), ())), preferred_element_type=f32)


def silu(v):
    return v / (1.0 + jnp.exp(-v))


def turned(values, cosine, sine):
    return (values * cosine + pltpu.roll(values, HEAD_SIZE // 2, 1) * sine).astype(bf16)


OPERANDS = (
    "hidden",
    "gain",
    "w_in",
    "w_gate",
    "conv_w",
    "conv_b",
    "conv_s",
    "w_state",
    "w_step",
    "step_b",
    "decay",
    "skip",
    "state",
    "w_out",
    "w_query",
    "w_key",
    "w_value",
    "w_attn",
    "m_gate",
    "m_up",
    "m_down",
    "cached",
    "lengths",
    "cosine",
    "sine",
)


def step_kernel(groups, seq_size, rank, tile, *refs):
    count = len(OPERANDS)
    hbm = dict(zip(OPERANDS, refs[:count]))
    out_ref, state_out_ref = refs[count : count + 2]
    held = dict(zip(OPERANDS, refs[count + 2 : 2 * count + 2]))
    (
        gathered,
        normed_ref,
        keys,
        values,
        query_rows,
        key_rows,
        value_rows,
        part_src,
        part_land,
        plane_src,
        plane_land,
        low_ref,
        step_ref,
        conv_ref,
        mix_ref,
        gate_ref,
        att_src,
        att_land,
        term,
        outgoing,
        landed,
        in_sem,
        x_sem,
        out_sem,
        gather_send,
        gather_recv,
        part_send,
        part_recv,
        plane_send,
        plane_recv,
        att_send,
        att_recv,
        sum_send,
        sum_recv,
    ) = refs[2 * count + 2 :]
    devices = groups * seq_size
    group = lax.axis_index("grp")
    place = lax.axis_index("seq")
    me = group * seq_size + place
    rows, width = held["hidden"].shape
    model = devices * width
    own, window, _ = held["cached"].shape
    kv_width = held["w_key"].shape[1]
    q_width = held["w_query"].shape[1]
    kv_here = kv_width // HEAD_SIZE
    heads = q_width // HEAD_SIZE
    per_kv = heads // kv_here
    state_size = held["decay"].shape[0]

    def group_at(dg):
        return lax.rem(group + dg, groups) if dg else group

    def place_at(ds):
        return lax.rem(place + ds, seq_size) if ds else place

    every = [
        (dg * seq_size + ds, (group_at(dg), place_at(ds)))
        for dg in range(groups)
        for ds in range(seq_size)
        if dg or ds
    ]
    plane = [(ds, (group, place_at(ds))) for ds in range(1, seq_size)]
    column = [(dg, (group_at(dg), place)) for dg in range(1, groups)]

    def remote(src, dst, send, recv, k, where):
        return pltpu.make_async_remote_copy(
            src_ref=src,
            dst_ref=dst,
            send_sem=send.at[k],
            recv_sem=recv.at[k],
            device_id=where,
            device_id_type=MESH,
        )

    barrier = pltpu.get_barrier_semaphore()
    for _, where in every:
        pl.semaphore_signal(barrier, inc=1, device_id=where, device_id_type=MESH)

    def load(name):
        return pltpu.make_async_copy(
            hbm[name], held[name], in_sem.at[OPERANDS.index(name)]
        )

    tiles = window // tile

    def load_x(b, t):
        at = (b, pl.ds(t * tile, tile))
        return pltpu.make_async_copy(
            hbm["cached"].at[at], held["cached"].at[at], x_sem.at[b * tiles + t]
        )

    def start(*names):
        for name in names:
            load(name).start()

    def finish(*names):
        for name in names:
            load(name).wait()

    start("hidden", "w_key")
    load_x(0, 0).start()
    start("w_value", "cosine", "sine", "lengths")
    for t in range(1, tiles):
        load_x(0, t).start()
    start("gain", "conv_w", "conv_b", "conv_s")
    for b in range(1, own):
        for t in range(tiles):
            load_x(b, t).start()
    later = ["w_in", "w_state", "w_gate", "w_query", "w_step", "step_b", "decay", "skip"]
    last = ["m_gate", "m_up", "m_down", "state", "w_attn", "w_out"]

    finish("w_key", "cosine", "sine")

    def project(b, t):
        load_x(b, t).wait()
        x = held["cached"][b, t * tile : (t + 1) * tile, :]
        slots = slice(t * tile, (t + 1) * tile)
        at = slice(b * window + t * tile, b * window + (t + 1) * tile)
        k_rows = dot_nn(x, held["w_key"][...])
        cosine, sine = held["cosine"][slots, :], held["sine"][slots, :]
        for h in range(kv_here):
            cols = slice(h * HEAD_SIZE, (h + 1) * HEAD_SIZE)
            keys[at, cols] = turned(k_rows[:, cols], cosine, sine)
        if b == 0 and t == 0:
            finish("w_value")
        v_rows = dot_nn(x, held["w_value"][...])
        values[at, :] = v_rows.astype(bf16)

    gather = [(k, where, remote(held["hidden"], gathered.at[me], gather_send, gather_recv, k, where)) for k, where in every]

    for b in range(own):
        for t in range(tiles):
            project(b, t)
            if b == 0 and t == 0:
                finish("hidden")
                pl.semaphore_wait(barrier, devices - 1)
                for _, _, copy in gather:
                    copy.start()
                gathered[me] = held["hidden"][...]
                start(*later)
        if b == 0:
            start(*last)

    finish("gain", "conv_w", "conv_b", "conv_s")
    past = held["conv_b"][...]
    for k in range(held["conv_s"].shape[0]):
        past = past + held["conv_s"][k].astype(f32) * held["conv_w"][k : k + 1, :]
    conv_ref[...] = past

    for _, _, copy in gather:
        copy.wait()
    total = jnp.zeros((rows, width), f32)
    for d in range(devices):
        block = gathered[d].astype(f32)
        total = total + block * block
    scale = lax.rsqrt(jnp.sum(total, axis=1, keepdims=True) * (1.0 / model) + epsilon)
    for d in range(devices):
        cols = slice(d * width, (d + 1) * width)
        normed_ref[:, cols] = (gathered[d].astype(f32) * scale * held["gain"][:, cols]).astype(bf16)

    finish("w_in", "w_state")
    normed = normed_ref[...]
    taps = held["conv_w"].shape[0]
    ssm_input = dot_nn(normed, held["w_in"][...]).astype(bf16).astype(f32)
    conv_out = silu(conv_ref[...] + held["conv_w"][taps - 1 : taps, :] * ssm_input)
    conv_ref[...] = conv_out
    part_src[...] = dot_nt(conv_out.astype(bf16), held["w_state"][...]).astype(bf16)

    part = [remote(part_src, part_land.at[place], part_send, part_recv, k, where) for k, where in plane]
    for copy in part:
        copy.start()
    part_land[place] = part_src[...]

    finish("w_query", "w_gate", "lengths")
    query_rows[...] = dot_nn(normed, held["w_query"][...])
    key_rows[...] = dot_nn(normed, held["w_key"][...])
    value_rows[...] = dot_nn(normed, held["w_value"][...])
    gate_ref[...] = silu(dot_nn(normed, held["w_gate"][...]))

    first = place * own
    score_scale = HEAD_SIZE ** (-0.5)
    padded = -(-heads // 8) * 8
    row_id = lax.broadcasted_iota(jnp.int32, (padded, HEAD_SIZE), 0)
    slot_id = lax.broadcasted_iota(jnp.int32, (padded, window), 1)

    def attend(b):
        length = held["lengths"][first + b]
        q_row = query_rows[pl.ds(first + b, 1), :]
        k_row = key_rows[pl.ds(first + b, 1), :]
        v_row = value_rows[pl.ds(first + b, 1), :]
        cosine = held["cosine"][pl.ds(length, 1), :]
        sine = held["sine"][pl.ds(length, 1), :]
        stacked = jnp.zeros((padded, HEAD_SIZE), f32)
        for q in range(heads):
            stacked = jnp.where(row_id == q, q_row[:, q * HEAD_SIZE : (q + 1) * HEAD_SIZE], stacked)
        query = turned(stacked, cosine, sine).astype(f32)
        wide = jnp.concatenate(
            [
                jnp.where((row_id >= h * per_kv) & (row_id < (h + 1) * per_kv), query, 0.0)
                for h in range(kv_here)
            ],
            axis=1,
        )
        fresh_key = jnp.concatenate(
            [
                turned(k_row[:, h * HEAD_SIZE : (h + 1) * HEAD_SIZE], cosine, sine).astype(f32)
                for h in range(kv_here)
            ],
            axis=1,
        )
        here = slice(b * window, (b + 1) * window)
        scores = dot_nt(wide.astype(bf16), keys[here, :]) * score_scale
        scores = jnp.where(slot_id < length, scores, -1e30)
        fresh = jnp.sum(wide * fresh_key, axis=1, keepdims=True) * score_scale
        top = jnp.maximum(jnp.max(scores, axis=1, keepdims=True), fresh)
        weights = jnp.exp(scores - top)
        weight_new = jnp.exp(fresh - top)
        total = jnp.sum(weights, axis=1, keepdims=True) + weight_new
        mixed = dot_nn(weights.astype(bf16), values[here, :])
        mixed = (mixed + weight_new * v_row.astype(bf16).astype(f32)) / total
        mixed = mixed.astype(bf16).astype(f32)
        for q in range(heads):
            h = q // per_kv
            att_src[b : b + 1, q * HEAD_SIZE : (q + 1) * HEAD_SIZE] = mixed[
                q : q + 1, h * HEAD_SIZE : (h + 1) * HEAD_SIZE
            ]

    for b in range(own):
        attend(b)

    att = [remote(att_src, att_land.at[place], att_send, att_recv, k, where) for k, where in plane]
    for copy in part:
        copy.wait()
    plane_sum = part_land[0].astype(f32)
    for s in range(1, seq_size):
        plane_sum = plane_sum + part_land[s].astype(f32)
    plane_src[...] = plane_sum
    crossing = [
        remote(plane_src, plane_land.at[group], plane_send, plane_recv, k, where) for k, where in column
    ]
    for copy in crossing:
        copy.start()
    for copy in att:
        copy.start()
    plane_land[group] = plane_sum
    att_land[place] = att_src[...]

    finish("m_gate", "m_up")
    hidden = (
        silu(dot_nt(normed, held["m_gate"][...])) * dot_nt(normed, held["m_up"][...])
    ).astype(bf16)
    finish("m_down", "w_attn")
    term[...] = dot_nn(hidden, held["m_down"][...])
    finish("w_step", "step_b", "decay", "skip", "state", "w_out")
    rate = jnp.exp(held["decay"][...])

    for copy in crossing:
        copy.wait()
    low = plane_land[0]
    for z in range(1, groups):
        low = low + plane_land[z]
    low_ref[...] = low
    raw = dot_nn(low[:, :rank].astype(bf16), held["w_step"][...]) + held["step_b"][...]
    step_ref[...] = jnp.maximum(raw, 0.0) + jnp.log1p(jnp.exp(-jnp.abs(raw)))

    def advance(i, carry):
        some = pl.ds(pl.multiple_of(i * 8, 8), 8)
        step = step_ref[some, :][:, None, :]
        conv = conv_ref[some, :][:, None, :]
        tail = low_ref[some, :]
        input_map = tail[:, rank : rank + state_size][:, :, None]
        output_map = tail[:, rank + state_size :][:, :, None]
        fresh = jnp.exp(-step * rate[None]) * held["state"][some] + (step * conv) * input_map
        held["state"][some] = fresh
        mix_ref[some, :] = jnp.sum(fresh * output_map, axis=1)
        return carry

    lax.fori_loop(0, rows // 8, advance, 0)
    mixed = mix_ref[...] + held["skip"][...] * conv_ref[...]
    ssm_gated = (mixed * gate_ref[...]).astype(bf16)

    for copy in att:
        copy.wait()
    attended = jnp.concatenate([att_land[s] for s in range(seq_size)], axis=0).astype(bf16)
    col_width = held["w_attn"].shape[1]
    cols = pl.ds(pl.multiple_of(place * col_width, col_width), col_width)
    term[:, cols] += dot_nn(attended, held["w_attn"][...])

    save = pltpu.make_async_copy(held["state"], state_out_ref, out_sem)
    save.start()

    chunk = seq_size * width
    order = sorted(range(groups), key=lambda dg: -min(dg, groups - dg))

    def leave(dg, ds):
        where = (group_at(dg), place_at(ds))
        return remote(
            outgoing.at[where[0] * seq_size + where[1]],
            landed.at[me],
            sum_send,
            sum_recv,
            dg * seq_size + ds,
            where,
        )

    for dg in order:
        base = group_at(dg)
        cols = pl.ds(pl.multiple_of(base * chunk, chunk), chunk)
        block = dot_nn(ssm_gated, held["w_out"][:, cols]) + term[:, cols]
        for s in range(seq_size):
            outgoing[base * seq_size + s] = block[:, s * width : (s + 1) * width].astype(bf16)
        for ds in range(seq_size):
            if dg or ds:
                leave(dg, ds).start()
    landed[me] = outgoing[me]
    for k, _ in every:
        leave(k // seq_size, k % seq_size).wait()
    total = landed[0].astype(f32)
    for d in range(1, devices):
        total = total + landed[d].astype(f32)
    out_ref[...] = (held["hidden"][...].astype(f32) + total).astype(bf16)
    save.wait()


def rotary_tables(count):
    half_dim = HEAD_SIZE // 2
    frequency = rope_base ** (-(np.arange(half_dim, dtype=np.float32) * 2.0) / HEAD_SIZE)
    angles = np.arange(count, dtype=np.float32)[:, None] * frequency.astype(np.float32)
    cosine, sine = np.cos(angles), np.sin(angles)
    return (
        np.concatenate([cosine, cosine], axis=1).astype(np.float32),
        np.concatenate([-sine, sine], axis=1).astype(np.float32),
    )


def per_device(
    groups,
    seq_size,
    hidden_in,
    norm_gain,
    w_ssm_in,
    w_ssm_gate,
    conv_weight,
    conv_bias,
    conv_state,
    w_state_proj,
    w_step,
    step_bias,
    log_decay,
    skip_gain,
    ssm_state,
    w_ssm_out,
    w_query,
    key_projection,
    value_projection,
    w_attn_out,
    w_mlp_gate,
    w_mlp_up,
    w_mlp_down,
    cached_inputs,
    window_lengths,
):
    rows, width = hidden_in.shape
    devices = groups * seq_size
    model = devices * width
    own, window, _ = cached_inputs.shape
    kv_width, q_width = key_projection.shape[1], w_query.shape[1]
    channels = w_ssm_in.shape[1]
    low_width = w_state_proj.shape[1]
    tile = 256 if window % 256 == 0 else window
    cosine, sine = rotary_tables(window + 8)
    operands = dict(
        hidden=hidden_in,
        gain=norm_gain.reshape(1, -1),
        w_in=w_ssm_in,
        w_gate=w_ssm_gate,
        conv_w=conv_weight,
        conv_b=conv_bias.reshape(1, -1),
        conv_s=conv_state.transpose(1, 0, 2),
        w_state=w_state_proj.T,
        w_step=w_step,
        step_b=step_bias.reshape(1, -1),
        decay=log_decay,
        skip=skip_gain.reshape(1, -1),
        state=ssm_state,
        w_out=w_ssm_out,
        w_query=w_query,
        w_key=key_projection,
        w_value=value_projection,
        w_attn=w_attn_out,
        m_gate=w_mlp_gate.T,
        m_up=w_mlp_up.T,
        m_down=w_mlp_down,
        cached=cached_inputs,
        lengths=window_lengths,
        cosine=jnp.asarray(cosine),
        sine=jnp.asarray(sine),
    )
    dma = pltpu.SemaphoreType.DMA
    any_spec = pl.BlockSpec(memory_space=pl.ANY)
    own_copies = [
        (pltpu.SMEM if name == "lengths" else pltpu.VMEM)(operands[name].shape, operands[name].dtype)
        for name in OPERANDS
    ]
    return pl.pallas_call(
        functools.partial(step_kernel, groups, seq_size, w_step.shape[0], tile),
        out_shape=(
            jax.ShapeDtypeStruct((rows, width), bf16),
            jax.ShapeDtypeStruct(ssm_state.shape, f32),
        ),
        in_specs=[any_spec] * len(OPERANDS),
        out_specs=(pl.BlockSpec(memory_space=pltpu.VMEM), any_spec),
        scratch_shapes=own_copies
        + [
            pltpu.VMEM((devices, rows, width), bf16),
            pltpu.VMEM((rows, model), bf16),
            pltpu.VMEM((own * window, kv_width), bf16),
            pltpu.VMEM((own * window, kv_width), bf16),
            pltpu.VMEM((rows, q_width), f32),
            pltpu.VMEM((rows, kv_width), f32),
            pltpu.VMEM((rows, kv_width), f32),
            pltpu.VMEM((rows, low_width), bf16),
            pltpu.VMEM((seq_size, rows, low_width), bf16),
            pltpu.VMEM((rows, low_width), f32),
            pltpu.VMEM((groups, rows, low_width), f32),
            pltpu.VMEM((rows, low_width), f32),
            pltpu.VMEM((rows, channels), f32),
            pltpu.VMEM((rows, channels), f32),
            pltpu.VMEM((rows, channels), f32),
            pltpu.VMEM((rows, channels), f32),
            pltpu.VMEM((own, q_width), f32),
            pltpu.VMEM((seq_size, own, q_width), f32),
            pltpu.VMEM((rows, model), f32),
            pltpu.VMEM((devices, rows, width), bf16),
            pltpu.VMEM((devices, rows, width), bf16),
            dma((len(OPERANDS),)),
            dma((own * window // tile,)),
            dma,
            dma((devices,)),
            dma((devices,)),
            dma((seq_size,)),
            dma((seq_size,)),
            dma((groups,)),
            dma((groups,)),
            dma((seq_size,)),
            dma((seq_size,)),
            dma((devices,)),
            dma((devices,)),
        ],
        compiler_params=pltpu.CompilerParams(
            collective_id=0, has_side_effects=True, vmem_limit_bytes=VMEM_LIMIT
        ),
    )(*[operands[name] for name in OPERANDS])


def solution(mesh):
    placed = (
        P(None, ("grp", "seq")),
        P(),
        P(None, ("grp", "seq")),
        P(None, ("grp", "seq")),
        P(None, ("grp", "seq")),
        P(("grp", "seq")),
        P(None, None, ("grp", "seq")),
        P(("grp", "seq"), None),
        P(None, ("grp", "seq")),
        P(("grp", "seq")),
        P(None, ("grp", "seq")),
        P(("grp", "seq")),
        P(None, None, ("grp", "seq")),
        P(("grp", "seq"), None),
        P(None, "grp"),
        P(None, "grp"),
        P(None, "grp"),
        P("grp", "seq"),
        P(None, ("grp", "seq")),
        P(None, ("grp", "seq")),
        P(("grp", "seq"), None),
        P("seq", None, None),
        P(),
    )
    return jax.shard_map(
        functools.partial(per_device, mesh.shape["grp"], mesh.shape["seq"]),
        mesh=mesh,
        in_specs=placed,
        out_specs=(P(None, ("grp", "seq")), P(None, None, ("grp", "seq"))),
        check_vma=False,
    )
```

time: 70 us -> 39.2 us (0.56)
  Pallas kernels: 50.2 us -> 35.3 us
  matrix products: 13 us -> 0 us
  other arithmetic: 3.32 us -> 0 us
  local copies, waits for them, and re-layouts: 2.21 us -> 3.05 us
    pallas_call x4 -> x1, Pallas kernels: 50.2 us -> 35.3 us  [per_device(): pl.pallas_call(functools.partial(step_kernel, groups, seq_size, w_step.sh...]
    dot_general x7 -> x0, matrix products: 13 us -> none  [the longest x1 5.08 us: per_device(): jnp.dot(mlp_hidden, w_mlp_down, preferred_element_type=jnp.float32)]
    neg x2 -> x0, other arithmetic: 1.11 us -> none  [rotary_tables(): -sine]
    reduce_sum x2 -> x0, other arithmetic: 0.94 us -> none  [the longest x1 0.93 us: per_device(): jnp.sum(state_out * output_map[:, :, None], axis=1) + skip_gain * conv_out]
    unnamed x33 -> x2, local copies, waits for them, and re-layouts: 2.13 us -> 3.05 us
    convert_element_type x2 -> x0, other arithmetic: 0.88 us -> none  [the longest x1 0.88 us: window_attention(): cos_new, sin_new = rotary_tables(lengths.astype(jnp.float32))]
where the time goes in v1:
time: 39.2 us; the launch traced here: 39 us
  Pallas kernels  35.3 us (90%)
  local copies, waits for them, and re-layouts  3.05 us (8%)
  between operations  0.65 us (2%)
    pallas_call x1, Pallas kernels, per_device(): pl.pallas_call(functools.partial(step_kernel, groups, seq_size, w_step.sh...  35.3 us
    unnamed x2, local copies, waits for them, and re-layouts  3.05 us

profile of v1, /device:TPU:0, one launch (start us, length us, event | category | flops | bytes accessed | tf_op | source)
XLA Modules:
  0.0 39.0 jit_solution(3023022032740130565)
XLA Ops:
  0.6 35.3 %shard_map.248 = (bf16[24,128]{1,0:T(8,128)(2,1)}, f32[24,16,256]{2,1,0:T(8,128)}) custom-call(bf16[24,128]{1,0:T(8,128)(2,1)} %refs_0_.1, f32[1,4096]{1,0:T(1,128)} %bitcast.12, bf16[4096,256]{1,0:T(8,128)(2,1)} %refs_2_.1, bf16[4096,256]{1,0:T(8,128)(2,1)} %refs_3_.1, f32[4,256]{1,0:T(4,128)} %refs_4_.1, f32[1,256]{1,0:T(1,128)} %bitcast.13, ...), custom_call_target="tpu_custom_call" | custom-call | tf_op jit(solution)/shard_map/pallas_call | solution.py:477
  36.0 1.3 %copy.29 = bf16[24,128]{1,0:T(8,128)(2,1)} copy(bf16[24,128]{1,0:T(8,128)(2,1)} %get-tuple-element.4) | data formatting | bytes 12288
  37.3 1.8 %copy.30 = f32[24,16,256]{2,1,0:T(8,128)} copy(f32[24,16,256]{2,1,0:T(8,128)} %get-tuple-element.5) | data formatting | bytes 786432

commit v2 on v1

--- a/solution.py
+++ b/solution.py
@@ -10,7 +10,9 @@
 
 HEAD_SIZE = 128
 MESH = pl.DeviceIdType.MESH
-VMEM_LIMIT = 66_000_000
+VMEM_LIMIT = 48 * 1024 * 1024
+LATE = 1
+MEET_LAST = 2
 
 epsilon = 1e-05
 rope_base = 10000.0
@@ -25,6 +27,11 @@
 
 def dot_nt(a, b):
     return lax.dot_general(a, b, (((1,), (1,)), ((), ())), preferred_element_type=f32)
+
+
+def dot_halves(a, b):
+    half = b.shape[0] // 2
+    return dot_nn(a[:, :half], b[:half, :]) + dot_nn(a[:, half:], b[half:, :])
 
 
 def silu(v):
@@ -93,17 +100,7 @@
         landed,
         in_sem,
         x_sem,
-        out_sem,
-        gather_send,
-        gather_recv,
-        part_send,
-        part_recv,
-        plane_send,
-        plane_recv,
-        att_send,
-        att_recv,
-        sum_send,
-        sum_recv,
+        link_sem,
     ) = refs[2 * count + 2 :]
     devices = groups * seq_size
     group = lax.axis_index("grp")
@@ -134,15 +131,21 @@
     plane = [(ds, (group, place_at(ds))) for ds in range(1, seq_size)]
     column = [(dg, (group_at(dg), place)) for dg in range(1, groups)]
 
-    def remote(src, dst, send, recv, k, where):
+    def remote(src, dst, pair, where):
         return pltpu.make_async_remote_copy(
             src_ref=src,
             dst_ref=dst,
-            send_sem=send.at[k],
-            recv_sem=recv.at[k],
+            send_sem=link_sem.at[2 * pair],
+            recv_sem=link_sem.at[2 * pair + 1],
             device_id=where,
             device_id_type=MESH,
         )
+
+    def await_sent(block, pair):
+        pltpu.make_async_copy(block, block, link_sem.at[2 * pair]).wait()
+
+    def await_landed(block, pair):
+        pltpu.make_async_copy(block, block, link_sem.at[2 * pair + 1]).wait()
 
     barrier = pltpu.get_barrier_semaphore()
     for _, where in every:
@@ -169,22 +172,46 @@
         for name in names:
             load(name).wait()
 
+    spans = [(b, t) for b in range(own) for t in range(tiles)]
+    waiting = [
+        ["gain", "conv_w", "conv_b", "conv_s", "lengths"],
+        ["w_in", "w_state"],
+        ["w_query", "w_gate"],
+        ["m_gate"],
+        ["m_up", "w_step", "step_b", "decay", "skip"],
+        ["m_down", "state", "w_attn", "w_out"],
+    ]
     start("hidden", "w_key")
-    load_x(0, 0).start()
-    start("w_value", "cosine", "sine", "lengths")
-    for t in range(1, tiles):
-        load_x(0, t).start()
-    start("gain", "conv_w", "conv_b", "conv_s")
-    for b in range(1, own):
-        for t in range(tiles):
-            load_x(b, t).start()
-    later = ["w_in", "w_state", "w_gate", "w_query", "w_step", "step_b", "decay", "skip"]
-    last = ["m_gate", "m_up", "m_down", "state", "w_attn", "w_out"]
-
-    finish("w_key", "cosine", "sine")
-
-    def project(b, t):
+    load_x(*spans[0]).start()
+    start("w_value", "cosine", "sine")
+
+    def meet():
+        with jax.named_scope("meet"):
+            finish("hidden")
+            pl.semaphore_wait(barrier, devices - 1)
+        for _, where in every:
+            remote(held["hidden"], gathered.at[me], 0, where).start()
+        gathered[me] = held["hidden"][...]
+
+    far = group == groups - 1
+    first_chip = jnp.logical_and(group == 0, place < 2)
+    middle = jnp.logical_not(jnp.logical_or(far, first_chip))
+    pl.when(far)(meet)
+    with jax.named_scope("first_wait"):
+        finish("w_key")
+
+    load_x(*spans[1]).start()
+
+    def project(i):
+        b, t = spans[i]
         load_x(b, t).wait()
+        if i == 0:
+            finish("w_value", "cosine", "sine")
+        if i + 2 < len(spans):
+            load_x(*spans[i + 2]).start()
+        last = len(waiting) if i + 1 == len(spans) else i + 1
+        for names in waiting[i:last]:
+            start(*names)
         x = held["cached"][b, t * tile : (t + 1) * tile, :]
         slots = slice(t * tile, (t + 1) * tile)
         at = slice(b * window + t * tile, b * window + (t + 1) * tile)
@@ -193,25 +220,18 @@
         for h in range(kv_here):
             cols = slice(h * HEAD_SIZE, (h + 1) * HEAD_SIZE)
             keys[at, cols] = turned(k_rows[:, cols], cosine, sine)
-        if b == 0 and t == 0:
-            finish("w_value")
         v_rows = dot_nn(x, held["w_value"][...])
         values[at, :] = v_rows.astype(bf16)
 
-    gather = [(k, where, remote(held["hidden"], gathered.at[me], gather_send, gather_recv, k, where)) for k, where in every]
-
-    for b in range(own):
-        for t in range(tiles):
-            project(b, t)
-            if b == 0 and t == 0:
-                finish("hidden")
-                pl.semaphore_wait(barrier, devices - 1)
-                for _, _, copy in gather:
-                    copy.start()
-                gathered[me] = held["hidden"][...]
-                start(*later)
-        if b == 0:
-            start(*last)
+
+    early = max(len(spans) - LATE, 1)
+    for i in range(early):
+        with jax.named_scope("project"):
+            project(i)
+        if i == 0:
+            pl.when(middle)(meet)
+        if i == min(early - 1, MEET_LAST):
+            pl.when(first_chip)(meet)
 
     finish("gain", "conv_w", "conv_b", "conv_s")
     past = held["conv_b"][...]
@@ -219,35 +239,41 @@
         past = past + held["conv_s"][k].astype(f32) * held["conv_w"][k : k + 1, :]
     conv_ref[...] = past
 
-    for _, _, copy in gather:
-        copy.wait()
-    total = jnp.zeros((rows, width), f32)
-    for d in range(devices):
-        block = gathered[d].astype(f32)
-        total = total + block * block
-    scale = lax.rsqrt(jnp.sum(total, axis=1, keepdims=True) * (1.0 / model) + epsilon)
-    for d in range(devices):
-        cols = slice(d * width, (d + 1) * width)
-        normed_ref[:, cols] = (gathered[d].astype(f32) * scale * held["gain"][:, cols]).astype(bf16)
-
-    finish("w_in", "w_state")
-    normed = normed_ref[...]
-    taps = held["conv_w"].shape[0]
-    ssm_input = dot_nn(normed, held["w_in"][...]).astype(bf16).astype(f32)
-    conv_out = silu(conv_ref[...] + held["conv_w"][taps - 1 : taps, :] * ssm_input)
-    conv_ref[...] = conv_out
-    part_src[...] = dot_nt(conv_out.astype(bf16), held["w_state"][...]).astype(bf16)
-
-    part = [remote(part_src, part_land.at[place], part_send, part_recv, k, where) for k, where in plane]
-    for copy in part:
-        copy.start()
+    with jax.named_scope("gather_wait"):
+        await_landed(gathered.at[pl.ds(0, devices - 1)], 0)
+
+    with jax.named_scope("norm"):
+        total = jnp.zeros((rows, width), f32)
+        for d in range(devices):
+            block = gathered[d].astype(f32)
+            total = total + block * block
+        scale = lax.rsqrt(jnp.sum(total, axis=1, keepdims=True) * (1.0 / model) + epsilon)
+        for d in range(devices):
+            cols = slice(d * width, (d + 1) * width)
+            normed_ref[:, cols] = (gathered[d].astype(f32) * scale * held["gain"][:, cols]).astype(bf16)
+
+    with jax.named_scope("ssm_in"):
+        finish("w_in", "w_state")
+        normed = normed_ref[...]
+        taps = held["conv_w"].shape[0]
+        ssm_input = dot_halves(normed, held["w_in"][...]).astype(bf16).astype(f32)
+        conv_out = silu(conv_ref[...] + held["conv_w"][taps - 1 : taps, :] * ssm_input)
+        conv_ref[...] = conv_out
+        part_src[...] = dot_nt(conv_out.astype(bf16), held["w_state"][...]).astype(bf16)
+
+    for _, where in plane:
+        remote(part_src, part_land.at[place], 1, where).start()
     part_land[place] = part_src[...]
 
-    finish("w_query", "w_gate", "lengths")
-    query_rows[...] = dot_nn(normed, held["w_query"][...])
-    key_rows[...] = dot_nn(normed, held["w_key"][...])
-    value_rows[...] = dot_nn(normed, held["w_value"][...])
-    gate_ref[...] = silu(dot_nn(normed, held["w_gate"][...]))
+    for i in range(early, len(spans)):
+        with jax.named_scope("project"):
+            project(i)
+    with jax.named_scope("qkv_gate"):
+        finish("w_query", "w_gate", "lengths")
+        query_rows[...] = dot_nn(normed, held["w_query"][...])
+        key_rows[...] = dot_nn(normed, held["w_key"][...])
+        value_rows[...] = dot_nn(normed, held["w_value"][...])
+        gate_ref[...] = silu(dot_nn(normed, held["w_gate"][...]))
 
     first = place * own
     score_scale = HEAD_SIZE ** (-0.5)
@@ -297,43 +323,45 @@
                 q : q + 1, h * HEAD_SIZE : (h + 1) * HEAD_SIZE
             ]
 
-    for b in range(own):
-        attend(b)
-
-    att = [remote(att_src, att_land.at[place], att_send, att_recv, k, where) for k, where in plane]
-    for copy in part:
-        copy.wait()
+    with jax.named_scope("attend"):
+        for b in range(own):
+            attend(b)
+
+    with jax.named_scope("part_wait"):
+        await_landed(part_land.at[pl.ds(0, seq_size - 1)], 1)
+
     plane_sum = part_land[0].astype(f32)
     for s in range(1, seq_size):
         plane_sum = plane_sum + part_land[s].astype(f32)
-    plane_src[...] = plane_sum
-    crossing = [
-        remote(plane_src, plane_land.at[group], plane_send, plane_recv, k, where) for k, where in column
-    ]
-    for copy in crossing:
-        copy.start()
-    for copy in att:
-        copy.start()
-    plane_land[group] = plane_sum
+    plane_src[...] = plane_sum.astype(bf16)
+    for _, where in column:
+        remote(plane_src, plane_land.at[group], 2, where).start()
+    for _, where in plane:
+        remote(att_src, att_land.at[place], 3, where).start()
+    plane_land[group] = plane_src[...]
     att_land[place] = att_src[...]
 
-    finish("m_gate", "m_up")
-    hidden = (
-        silu(dot_nt(normed, held["m_gate"][...])) * dot_nt(normed, held["m_up"][...])
-    ).astype(bf16)
-    finish("m_down", "w_attn")
-    term[...] = dot_nn(hidden, held["m_down"][...])
+    with jax.named_scope("mlp"):
+        finish("m_gate", "m_up")
+        hidden = (
+            silu(dot_nt(normed, held["m_gate"][...])) * dot_nt(normed, held["m_up"][...])
+        ).astype(bf16)
+        finish("m_down", "w_attn")
+        term[...] = dot_nn(hidden, held["m_down"][...])
+
     finish("w_step", "step_b", "decay", "skip", "state", "w_out")
     rate = jnp.exp(held["decay"][...])
 
-    for copy in crossing:
-        copy.wait()
-    low = plane_land[0]
-    for z in range(1, groups):
-        low = low + plane_land[z]
-    low_ref[...] = low
-    raw = dot_nn(low[:, :rank].astype(bf16), held["w_step"][...]) + held["step_b"][...]
-    step_ref[...] = jnp.maximum(raw, 0.0) + jnp.log1p(jnp.exp(-jnp.abs(raw)))
+    with jax.named_scope("cross_wait"):
+        await_landed(plane_land.at[pl.ds(0, groups - 1)], 2)
+
+    with jax.named_scope("step_size"):
+        low = plane_land[0].astype(f32)
+        for z in range(1, groups):
+            low = low + plane_land[z].astype(f32)
+        low_ref[...] = low
+        raw = dot_nn(low[:, :rank].astype(bf16), held["w_step"][...]) + held["step_b"][...]
+        step_ref[...] = jnp.maximum(raw, 0.0) + jnp.log1p(jnp.exp(-jnp.abs(raw)))
 
     def advance(i, carry):
         some = pl.ds(pl.multiple_of(i * 8, 8), 8)
@@ -343,23 +371,23 @@
         input_map = tail[:, rank : rank + state_size][:, :, None]
         output_map = tail[:, rank + state_size :][:, :, None]
         fresh = jnp.exp(-step * rate[None]) * held["state"][some] + (step * conv) * input_map
-        held["state"][some] = fresh
+        state_out_ref[some] = fresh
         mix_ref[some, :] = jnp.sum(fresh * output_map, axis=1)
         return carry
 
-    lax.fori_loop(0, rows // 8, advance, 0)
-    mixed = mix_ref[...] + held["skip"][...] * conv_ref[...]
-    ssm_gated = (mixed * gate_ref[...]).astype(bf16)
-
-    for copy in att:
-        copy.wait()
-    attended = jnp.concatenate([att_land[s] for s in range(seq_size)], axis=0).astype(bf16)
-    col_width = held["w_attn"].shape[1]
-    cols = pl.ds(pl.multiple_of(place * col_width, col_width), col_width)
-    term[:, cols] += dot_nn(attended, held["w_attn"][...])
-
-    save = pltpu.make_async_copy(held["state"], state_out_ref, out_sem)
-    save.start()
+    with jax.named_scope("advance"):
+        lax.fori_loop(0, rows // 8, advance, 0)
+        mixed = mix_ref[...] + held["skip"][...] * conv_ref[...]
+        ssm_gated = (mixed * gate_ref[...]).astype(bf16)
+
+    with jax.named_scope("att_wait"):
+        await_landed(att_land.at[pl.ds(0, seq_size - 1)], 3)
+
+    with jax.named_scope("attn_out"):
+        attended = jnp.concatenate([att_land[s] for s in range(seq_size)], axis=0).astype(bf16)
+        col_width = held["w_attn"].shape[1]
+        cols = pl.ds(pl.multiple_of(place * col_width, col_width), col_width)
+        term[:, cols] += dot_nn(attended, held["w_attn"][...])
 
     chunk = seq_size * width
     order = sorted(range(groups), key=lambda dg: -min(dg, groups - dg))
@@ -369,29 +397,46 @@
         return remote(
             outgoing.at[where[0] * seq_size + where[1]],
             landed.at[me],
-            sum_send,
-            sum_recv,
-            dg * seq_size + ds,
+            4,
             where,
         )
 
-    for dg in order:
-        base = group_at(dg)
-        cols = pl.ds(pl.multiple_of(base * chunk, chunk), chunk)
-        block = dot_nn(ssm_gated, held["w_out"][:, cols]) + term[:, cols]
-        for s in range(seq_size):
-            outgoing[base * seq_size + s] = block[:, s * width : (s + 1) * width].astype(bf16)
-        for ds in range(seq_size):
-            if dg or ds:
-                leave(dg, ds).start()
+    with jax.named_scope("ssm_out"):
+        for dg in order:
+            base = group_at(dg)
+            cols = pl.ds(pl.multiple_of(base * chunk, chunk), chunk)
+            block = dot_nn(ssm_gated, held["w_out"][:, cols]) + term[:, cols]
+            for s in range(seq_size):
+                outgoing[base * seq_size + s] = block[:, s * width : (s + 1) * width].astype(bf16)
+            for ds in range(seq_size):
+                if dg or ds:
+                    leave(dg, ds).start()
+
     landed[me] = outgoing[me]
-    for k, _ in every:
-        leave(k // seq_size, k % seq_size).wait()
-    total = landed[0].astype(f32)
-    for d in range(1, devices):
-        total = total + landed[d].astype(f32)
-    out_ref[...] = (held["hidden"][...].astype(f32) + total).astype(bf16)
-    save.wait()
+    with jax.named_scope("sum_wait"):
+        await_landed(landed.at[pl.ds(0, devices - 1)], 4)
+
+    with jax.named_scope("final"):
+        total = landed[0].astype(f32)
+        for d in range(1, devices):
+            total = total + landed[d].astype(f32)
+        out_ref[...] = (held["hidden"][...].astype(f32) + total).astype(bf16)
+    await_sent(gathered.at[pl.ds(0, devices - 1)], 0)
+    await_sent(part_land.at[pl.ds(0, seq_size - 1)], 1)
+    await_sent(plane_land.at[pl.ds(0, groups - 1)], 2)
+    await_sent(att_land.at[pl.ds(0, seq_size - 1)], 3)
+    await_sent(landed.at[pl.ds(0, devices - 1)], 4)
+
+
+def store_kernel(hidden_ref, state_ref, hidden_out, state_out, sem):
+    copies = [
+        pltpu.make_async_copy(state_ref, state_out, sem.at[0]),
+        pltpu.make_async_copy(hidden_ref, hidden_out, sem.at[1]),
+    ]
+    for copy in copies:
+        copy.start()
+    for copy in copies:
+        copy.wait()
 
 
 def rotary_tables(count):
@@ -469,19 +514,20 @@
         sine=jnp.asarray(sine),
     )
     dma = pltpu.SemaphoreType.DMA
-    any_spec = pl.BlockSpec(memory_space=pl.ANY)
+    hbm_spec = pl.BlockSpec(memory_space=pltpu.HBM)
+    vmem_spec = pl.BlockSpec(memory_space=pltpu.VMEM)
     own_copies = [
         (pltpu.SMEM if name == "lengths" else pltpu.VMEM)(operands[name].shape, operands[name].dtype)
         for name in OPERANDS
     ]
-    return pl.pallas_call(
+    hidden_out, state_out = pl.pallas_call(
         functools.partial(step_kernel, groups, seq_size, w_step.shape[0], tile),
         out_shape=(
             jax.ShapeDtypeStruct((rows, width), bf16),
             jax.ShapeDtypeStruct(ssm_state.shape, f32),
         ),
-        in_specs=[any_spec] * len(OPERANDS),
-        out_specs=(pl.BlockSpec(memory_space=pltpu.VMEM), any_spec),
+        in_specs=[hbm_spec] * len(OPERANDS),
+        out_specs=(vmem_spec, vmem_spec),
         scratch_shapes=own_copies
         + [
             pltpu.VMEM((devices, rows, width), bf16),
@@ -493,8 +539,8 @@
             pltpu.VMEM((rows, kv_width), f32),
             pltpu.VMEM((rows, low_width), bf16),
             pltpu.VMEM((seq_size, rows, low_width), bf16),
-            pltpu.VMEM((rows, low_width), f32),
-            pltpu.VMEM((groups, rows, low_width), f32),
+            pltpu.VMEM((rows, low_width), bf16),
+            pltpu.VMEM((groups, rows, low_width), bf16),
             pltpu.VMEM((rows, low_width), f32),
             pltpu.VMEM((rows, channels), f32),
             pltpu.VMEM((rows, channels), f32),
@@ -507,22 +553,23 @@
             pltpu.VMEM((devices, rows, width), bf16),
             dma((len(OPERANDS),)),
             dma((own * window // tile,)),
-            dma,
-            dma((devices,)),
-            dma((devices,)),
-            dma((seq_size,)),
-            dma((seq_size,)),
-            dma((groups,)),
-            dma((groups,)),
-            dma((seq_size,)),
-            dma((seq_size,)),
-            dma((devices,)),
-            dma((devices,)),
+            dma((10,)),
         ],
         compiler_params=pltpu.CompilerParams(
             collective_id=0, has_side_effects=True, vmem_limit_bytes=VMEM_LIMIT
         ),
-    )(*[operands[name] for name in OPERANDS])
+    )(*[pltpu.with_memory_space_constraint(operands[name], pltpu.HBM) for name in OPERANDS])
+    return pl.pallas_call(
+        store_kernel,
+        out_shape=(
+            jax.ShapeDtypeStruct((rows, width), bf16),
+            jax.ShapeDtypeStruct(ssm_state.shape, f32),
+        ),
+        in_specs=[vmem_spec] * 2,
+        out_specs=(hbm_spec, hbm_spec),
+        scratch_shapes=[dma((2,))],
+        compiler_params=pltpu.CompilerParams(vmem_limit_bytes=1024 * 1024),
+    )(hidden_out, state_out)
 
 
 def solution(mesh):

time: 39.2 us -> 31.2 us (0.80)
  Pallas kernels: 35.3 us -> 30.4 us
  local copies, waits for them, and re-layouts: 3.05 us -> 0 us
    pallas_call x1, Pallas kernels: 35.3 us -> 29.6 us  [per_device(): pl.pallas_call(functools.partial(step_kernel, groups, seq_size, w_step.sh...]
    unnamed x2 -> x0, local copies, waits for them, and re-layouts: 3.05 us -> none
    pallas_call x0 -> x1, Pallas kernels: none -> 0.77 us  [per_device(): pl.pallas_call(store_kernel, out_shape=(jax.ShapeDtypeStruct((rows, width...]
where the time goes in v2:
time: 31.2 us; the launch traced here: 31.1 us
  Pallas kernels  30.4 us (97%)
  between operations  0.65 us (2%)
    pallas_call x1, Pallas kernels, per_device(): pl.pallas_call(functools.partial(step_kernel, groups, seq_size, w_step.sh...  29.6 us
    pallas_call x1, Pallas kernels, per_device(): pl.pallas_call(store_kernel, out_shape=(jax.ShapeDtypeStruct((rows, width...  0.77 us

profile of v2, /device:TPU:0, one launch (start us, length us, event | category | flops | bytes accessed | tf_op | source)
XLA Modules:
  0.0 31.1 jit_solution(1381317626337783830)
XLA Ops:
  0.6 29.6 %shard_map.248 = (bf16[24,128]{1,0:T(8,128)(2,1)S(1)}, f32[24,16,256]{2,1,0:T(8,128)S(1)}) custom-call(bf16[24,128]{1,0:T(8,128)(2,1)} %refs_0_.1, f32[1,4096]{1,0:T(1,128)} %bitcast.12, bf16[4096,256]{1,0:T(8,128)(2,1)} %refs_2_.1, bf16[4096,256]{1,0:T(8,128)(2,1)} %refs_3_.1, f32[4,256]{1,0:T(4,128)} %refs_4_.1, f32[1,256]{1,0:T(1,128)} %bitcast.13, ...), custom_call_target="tpu_custom_call" | custom-call | tf_op jit(solution)/shard_map/pallas_call | solution.py:523
  30.3 0.8 %shard_map.249 = (bf16[24,128]{1,0:T(8,128)(2,1)}, f32[24,16,256]{2,1,0:T(8,128)}) custom-call(bf16[24,128]{1,0:T(8,128)(2,1)S(1)} %get-tuple-element.4.hidden_ref, f32[24,16,256]{2,1,0:T(8,128)S(1)} %get-tuple-element.5.state_ref), custom_call_target="tpu_custom_call" | custom-call | tf_op jit(solution)/shard_map/pallas_call | solution.py:562

commit v3 on v2

--- a/solution.py
+++ b/solution.py
@@ -12,7 +12,14 @@
 MESH = pl.DeviceIdType.MESH
 VMEM_LIMIT = 48 * 1024 * 1024
 LATE = 1
-MEET_LAST = 2
+MEET_LAST = 3
+AHEAD = 4
+PAIR = 2
+
+
+def GATHER_ORDER(groups):
+    return list(range(groups))
+
 
 epsilon = 1e-05
 rope_base = 10000.0
@@ -29,9 +36,12 @@
     return lax.dot_general(a, b, (((1,), (1,)), ((), ())), preferred_element_type=f32)
 
 
-def dot_halves(a, b):
-    half = b.shape[0] // 2
-    return dot_nn(a[:, :half], b[:half, :]) + dot_nn(a[:, half:], b[half:, :])
+def row_spans(own, window, tile):
+    spans = [(b, at, tile) for b in range(own) for at in range(0, window, tile)]
+    if tile % 2 == 0:
+        b, at, size = spans[0]
+        spans[:1] = [(b, at, size // 2), (b, at + size // 2, size // 2)]
+    return spans
 
 
 def silu(v):
@@ -98,6 +108,7 @@
         term,
         outgoing,
         landed,
+        halves_ref,
         in_sem,
         x_sem,
         link_sem,
@@ -124,7 +135,7 @@
 
     every = [
         (dg * seq_size + ds, (group_at(dg), place_at(ds)))
-        for dg in range(groups)
+        for dg in GATHER_ORDER(groups)
         for ds in range(seq_size)
         if dg or ds
     ]
@@ -156,12 +167,13 @@
             hbm[name], held[name], in_sem.at[OPERANDS.index(name)]
         )
 
-    tiles = window // tile
-
-    def load_x(b, t):
-        at = (b, pl.ds(t * tile, tile))
+    spans = row_spans(own, window, tile)
+
+    def load_x(i):
+        b, at, size = spans[i]
+        part = (b, pl.ds(at, size))
         return pltpu.make_async_copy(
-            hbm["cached"].at[at], held["cached"].at[at], x_sem.at[b * tiles + t]
+            hbm["cached"].at[part], held["cached"].at[part], x_sem.at[i]
         )
 
     def start(*names):
@@ -172,49 +184,61 @@
         for name in names:
             load(name).wait()
 
-    spans = [(b, t) for b in range(own) for t in range(tiles)]
     waiting = [
+        [],
+        [],
         ["gain", "conv_w", "conv_b", "conv_s", "lengths"],
         ["w_in", "w_state"],
         ["w_query", "w_gate"],
-        ["m_gate"],
-        ["m_up", "w_step", "step_b", "decay", "skip"],
+        ["m_gate", "m_up", "w_step", "step_b", "decay", "skip"],
         ["m_down", "state", "w_attn", "w_out"],
     ]
     start("hidden", "w_key")
-    load_x(*spans[0]).start()
+    load_x(0).start()
     start("w_value", "cosine", "sine")
+    load_x(1).start()
 
     def meet():
         with jax.named_scope("meet"):
             finish("hidden")
             pl.semaphore_wait(barrier, devices - 1)
-        for _, where in every:
-            remote(held["hidden"], gathered.at[me], 0, where).start()
+        for n in range(groups):
+            z = jnp.where(2 * group < groups, groups - 1 - n, n)
+            for ds in range(seq_size):
+                def go():
+                    remote(held["hidden"], gathered.at[me], 0, (z, place_at(ds))).start()
+                if ds:
+                    go()
+                else:
+                    pl.when(z != group)(go)
         gathered[me] = held["hidden"][...]
 
-    far = group == groups - 1
+    far = group >= groups // 2
     first_chip = jnp.logical_and(group == 0, place < 2)
     middle = jnp.logical_not(jnp.logical_or(far, first_chip))
     pl.when(far)(meet)
     with jax.named_scope("first_wait"):
         finish("w_key")
 
-    load_x(*spans[1]).start()
-
-    def project(i):
-        b, t = spans[i]
-        load_x(b, t).wait()
+    ahead = min(AHEAD, len(spans))
+    for n in range(2, ahead):
+        load_x(n).start()
+
+    def ready(i):
+        load_x(i).wait()
         if i == 0:
             finish("w_value", "cosine", "sine")
-        if i + 2 < len(spans):
-            load_x(*spans[i + 2]).start()
+        if i + ahead < len(spans):
+            load_x(i + ahead).start()
         last = len(waiting) if i + 1 == len(spans) else i + 1
         for names in waiting[i:last]:
             start(*names)
-        x = held["cached"][b, t * tile : (t + 1) * tile, :]
-        slots = slice(t * tile, (t + 1) * tile)
-        at = slice(b * window + t * tile, b * window + (t + 1) * tile)
+
+    def project(i):
+        b, begin, size = spans[i]
+        slots = slice(begin, begin + size)
+        x = held["cached"][b, slots, :]
+        at = slice(b * window + begin, b * window + begin + size)
         k_rows = dot_nn(x, held["w_key"][...])
         cosine, sine = held["cosine"][slots, :], held["sine"][slots, :]
         for h in range(kv_here):
@@ -225,15 +249,21 @@
 
 
     early = max(len(spans) - LATE, 1)
-    for i in range(early):
+    i = 0
+    while i < early:
+        some = range(i, min(early, i + (PAIR if i else 1)))
+        for n in some:
+            ready(n)
         with jax.named_scope("project"):
-            project(i)
+            for n in some:
+                project(n)
         if i == 0:
             pl.when(middle)(meet)
-        if i == min(early - 1, MEET_LAST):
+        i = some[-1] + 1
+        if some[0] <= MEET_LAST < i or (i == early and MEET_LAST >= i):
             pl.when(first_chip)(meet)
 
-    finish("gain", "conv_w", "conv_b", "conv_s")
+    finish("gain", "conv_w", "conv_b", "conv_s", "w_in", "w_state")
     past = held["conv_b"][...]
     for k in range(held["conv_s"].shape[0]):
         past = past + held["conv_s"][k].astype(f32) * held["conv_w"][k : k + 1, :]
@@ -253,10 +283,12 @@
             normed_ref[:, cols] = (gathered[d].astype(f32) * scale * held["gain"][:, cols]).astype(bf16)
 
     with jax.named_scope("ssm_in"):
-        finish("w_in", "w_state")
         normed = normed_ref[...]
         taps = held["conv_w"].shape[0]
-        ssm_input = dot_halves(normed, held["w_in"][...]).astype(bf16).astype(f32)
+        k_half = model // 2
+        halves_ref[0] = dot_nn(normed[:, :k_half], held["w_in"][:k_half, :])
+        halves_ref[1] = dot_nn(normed[:, k_half:], held["w_in"][k_half:, :])
+        ssm_input = (halves_ref[0] + halves_ref[1]).astype(bf16).astype(f32)
         conv_out = silu(conv_ref[...] + held["conv_w"][taps - 1 : taps, :] * ssm_input)
         conv_ref[...] = conv_out
         part_src[...] = dot_nt(conv_out.astype(bf16), held["w_state"][...]).astype(bf16)
@@ -266,10 +298,11 @@
     part_land[place] = part_src[...]
 
     for i in range(early, len(spans)):
-        with jax.named_scope("project"):
+        ready(i)
+    finish("w_query", "w_gate", "lengths")
+    with jax.named_scope("qkv_gate"):
+        for i in range(early, len(spans)):
             project(i)
-    with jax.named_scope("qkv_gate"):
-        finish("w_query", "w_gate", "lengths")
         query_rows[...] = dot_nn(normed, held["w_query"][...])
         key_rows[...] = dot_nn(normed, held["w_key"][...])
         value_rows[...] = dot_nn(normed, held["w_value"][...])
@@ -323,30 +356,29 @@
                 q : q + 1, h * HEAD_SIZE : (h + 1) * HEAD_SIZE
             ]
 
-    with jax.named_scope("attend"):
-        for b in range(own):
+    for b in range(own - 1):
+        with jax.named_scope("attend"):
             attend(b)
-
     with jax.named_scope("part_wait"):
         await_landed(part_land.at[pl.ds(0, seq_size - 1)], 1)
-
     plane_sum = part_land[0].astype(f32)
     for s in range(1, seq_size):
         plane_sum = plane_sum + part_land[s].astype(f32)
     plane_src[...] = plane_sum.astype(bf16)
+    plane_land[group] = plane_src[...]
     for _, where in column:
         remote(plane_src, plane_land.at[group], 2, where).start()
+    with jax.named_scope("attend"):
+        attend(own - 1)
     for _, where in plane:
         remote(att_src, att_land.at[place], 3, where).start()
-    plane_land[group] = plane_src[...]
     att_land[place] = att_src[...]
 
     with jax.named_scope("mlp"):
-        finish("m_gate", "m_up")
+        finish("m_gate", "m_up", "m_down", "w_attn")
         hidden = (
             silu(dot_nt(normed, held["m_gate"][...])) * dot_nt(normed, held["m_up"][...])
         ).astype(bf16)
-        finish("m_down", "w_attn")
         term[...] = dot_nn(hidden, held["m_down"][...])
 
     finish("w_step", "step_b", "decay", "skip", "state", "w_out")
@@ -551,8 +583,9 @@
             pltpu.VMEM((rows, model), f32),
             pltpu.VMEM((devices, rows, width), bf16),
             pltpu.VMEM((devices, rows, width), bf16),
+            pltpu.VMEM((2, rows, channels), f32),
             dma((len(OPERANDS),)),
-            dma((own * window // tile,)),
+            dma((len(row_spans(own, window, tile)),)),
             dma((10,)),
         ],
         compiler_params=pltpu.CompilerParams(

time: 31.2 us -> 30.9 us (level)
    pallas_call x1, Pallas kernels: 29.6 us -> 29.3 us  [per_device(): pl.pallas_call(functools.partial(step_kernel, groups, seq_size, w_step.sh...]
where the time goes in v3:
time: 30.9 us; the launch traced here: 30.7 us
  Pallas kernels  30.1 us (97%)
  between operations  0.65 us (2%)
    pallas_call x1, Pallas kernels, per_device(): pl.pallas_call(functools.partial(step_kernel, groups, seq_size, w_step.sh...  29.3 us
    pallas_call x1, Pallas kernels, per_device(): pl.pallas_call(store_kernel, out_shape=(jax.ShapeDtypeStruct((rows, width...  0.77 us

profile of v3, /device:TPU:0, one launch (start us, length us, event | category | flops | bytes accessed | tf_op | source)
XLA Modules:
  0.0 30.7 jit_solution(16025437240631280856)
XLA Ops:
  0.6 29.3 %shard_map.248 = (bf16[24,128]{1,0:T(8,128)(2,1)S(1)}, f32[24,16,256]{2,1,0:T(8,128)S(1)}) custom-call(bf16[24,128]{1,0:T(8,128)(2,1)} %refs_0_.1, f32[1,4096]{1,0:T(1,128)} %bitcast.12, bf16[4096,256]{1,0:T(8,128)(2,1)} %refs_2_.1, bf16[4096,256]{1,0:T(8,128)(2,1)} %refs_3_.1, f32[4,256]{1,0:T(4,128)} %refs_4_.1, f32[1,256]{1,0:T(1,128)} %bitcast.13, ...), custom_call_target="tpu_custom_call" | custom-call | tf_op jit(solution)/shard_map/pallas_call | solution.py:555
  30.0 0.8 %shard_map.249 = (bf16[24,128]{1,0:T(8,128)(2,1)}, f32[24,16,256]{2,1,0:T(8,128)}) custom-call(bf16[24,128]{1,0:T(8,128)(2,1)S(1)} %get-tuple-element.4.hidden_ref, f32[24,16,256]{2,1,0:T(8,128)S(1)} %get-tuple-element.5.state_ref), custom_call_target="tpu_custom_call" | custom-call | tf_op jit(solution)/shard_map/pallas_call | solution.py:595

commit v4 on v3

--- a/solution.py
+++ b/solution.py
@@ -422,28 +422,28 @@
         term[:, cols] += dot_nn(attended, held["w_attn"][...])
 
     chunk = seq_size * width
-    order = sorted(range(groups), key=lambda dg: -min(dg, groups - dg))
-
-    def leave(dg, ds):
-        where = (group_at(dg), place_at(ds))
-        return remote(
+    def leave(z, ds):
+        where = (z, place_at(ds))
+        remote(
             outgoing.at[where[0] * seq_size + where[1]],
             landed.at[me],
             4,
             where,
-        )
-
+        ).start()
+
+    low_half = 2 * group < groups
+    ahead_of = list(reversed(range(groups)))
     with jax.named_scope("ssm_out"):
-        for dg in order:
-            base = group_at(dg)
+        for dg in ahead_of:
+            step_up = jnp.where(low_half, dg, (groups - dg) % groups)
+            base = lax.rem(group + step_up, groups)
             cols = pl.ds(pl.multiple_of(base * chunk, chunk), chunk)
             block = dot_nn(ssm_gated, held["w_out"][:, cols]) + term[:, cols]
             for s in range(seq_size):
                 outgoing[base * seq_size + s] = block[:, s * width : (s + 1) * width].astype(bf16)
             for ds in range(seq_size):
                 if dg or ds:
-                    leave(dg, ds).start()
-
+                    leave(base, ds)
     landed[me] = outgoing[me]
     with jax.named_scope("sum_wait"):
         await_landed(landed.at[pl.ds(0, devices - 1)], 4)

time: 30.9 us -> 30.6 us (level)
  no operation moved by 1% of the time
where the time goes in v4:
time: 30.6 us; the launch traced here: 30.5 us
  Pallas kernels  29.8 us (97%)
  between operations  0.65 us (2%)
    pallas_call x1, Pallas kernels, per_device(): pl.pallas_call(functools.partial(step_kernel, groups, seq_size, w_step.sh...  29 us
    pallas_call x1, Pallas kernels, per_device(): pl.pallas_call(store_kernel, out_shape=(jax.ShapeDtypeStruct((rows, width...  0.77 us

profile of v4, /device:TPU:0, one launch (start us, length us, event | category | flops | bytes accessed | tf_op | source)
XLA Modules:
  0.0 30.5 jit_solution(1697785553207330451)
XLA Ops:
  0.6 29.0 %shard_map.248 = (bf16[24,128]{1,0:T(8,128)(2,1)S(1)}, f32[24,16,256]{2,1,0:T(8,128)S(1)}) custom-call(bf16[24,128]{1,0:T(8,128)(2,1)} %refs_0_.1, f32[1,4096]{1,0:T(1,128)} %bitcast.12, bf16[4096,256]{1,0:T(8,128)(2,1)} %refs_2_.1, bf16[4096,256]{1,0:T(8,128)(2,1)} %refs_3_.1, f32[4,256]{1,0:T(4,128)} %refs_4_.1, f32[1,256]{1,0:T(1,128)} %bitcast.13, ...), custom_call_target="tpu_custom_call" | custom-call | tf_op jit(solution)/shard_map/pallas_call | solution.py:555
  29.7 0.8 %shard_map.249 = (bf16[24,128]{1,0:T(8,128)(2,1)}, f32[24,16,256]{2,1,0:T(8,128)}) custom-call(bf16[24,128]{1,0:T(8,128)(2,1)S(1)} %get-tuple-element.4.hidden_ref, f32[24,16,256]{2,1,0:T(8,128)S(1)} %get-tuple-element.5.state_ref), custom_call_target="tpu_custom_call" | custom-call | tf_op jit(solution)/shard_map/pallas_call | solution.py:595
